TPU v7x, 32 devices: a whole 2x2x4 slice. The times are simulated.
32 devices in a mesh: groups: 2 (over y), seq: 4 (over z), head: 4 (over x, core).
Axes of the slice: x: 2, y: 2, z: 4, core: 2. Of those that a mesh axis runs over, the one named last changes fastest.
Arguments:
- residual: bfloat16 [1024, 2048], P(('groups', 'seq')), parts along dimension 0, may hold values from -6 to 6
- query_in: bfloat16 [1024, 2048], P(('groups', 'seq'), 'head'), parts along dimension 0, may hold values from -6 to 6
- key_in: bfloat16 [1024, 2048], P(('groups', 'seq'), 'head'), parts along dimension 0, may hold values from -6 to 6
- value_in: bfloat16 [1024, 4096], P(('groups', 'seq'), 'head'), parts along dimension 0, may hold values from -6 to 6
- gating_in: bfloat16 [1024, 4096], P(('groups', 'seq'), 'head'), parts along dimension 0, may hold values from -6 to 6
- beta_logit: float32 [1024, 32], P(('groups', 'seq'), 'head'), parts along dimension 0, may hold values from -12 to 2
- decay_logit: float32 [1024, 32], P(('groups', 'seq'), 'head'), parts along dimension 0, may hold values from -16 to 1
- seq_length: int32 [2], P('groups'), parts along dimension 0, may hold values from 256 to 512
- conv_query: float32 [4, 2048], P(None, 'head'), may hold values from -3 to 3
- conv_key: float32 [4, 2048], P(None, 'head'), may hold values from -3 to 3
- conv_value: float32 [4, 4096], P(None, 'head'), may hold values from -3 to 3
- decay_rate: float32 [32], P('head'), may hold values from 0.5 to 17
- norm_gain: float32 [128], replicated, may hold values from 0.1 to 1.9
- out_weight: bfloat16 [4096, 2048], P('head'), may hold values from -0.09375 to 0.09375
- attn_gain: float32 [2048], replicated, may hold values from 0.1 to 1.9
- query_weight: bfloat16 [2048, 8192], P('seq', 'head'), may hold values from -1 to 1
- key_value_weight: bfloat16 [2048, 1024], P('seq'), may hold values from -10 to 10
Outputs:
- hidden_out: bfloat16 [1024, 2048], P(('groups', 'seq')), parts along dimension 0
- attention_out: bfloat16 [1024, 4096], P(('groups', 'seq'), 'head'), parts along dimension 0
There are 2 independent parts, one for each index of `groups`. A program takes and returns all parts, laid end to end along the dimension named above; an argument that names none is the same for every part. Nothing has to cross between parts.
All inputs are finite; a program needn't handle non-finite values.
Results may differ from a plain program's by a relative error of at most 0.02.
The roundings to bfloat16 on the way count: a program that leaves them out, or rounds other values in their place, can miss the bound.
Values may be sent and summed in bfloat16 or wider, within the bound.
A program may use at most 128 MiB of HBM per device.

v0:
```python
import functools

import jax
import jax.numpy as jnp
from jax import lax
from jax.experimental import pallas as pl
from jax.experimental.pallas import tpu as pltpu
from jax.sharding import PartitionSpec as P

DK = 128
DV = 128
QUERY_HEADS = 16
KEY_VALUE_HEADS = 2
HEAD_WIDTH = 256
CONV = 4
PAD = 8

EPSILON = 1e-06
NEGATIVE = -1e30
MESH = pl.DeviceIdType.MESH
HIGHEST = lax.Precision.HIGHEST


def mm(a, b, contract=((1,), (0,))):
    return lax.dot_general(
        a, b, (contract, ((), ())), precision=HIGHEST, preferred_element_type=jnp.float32
    )


def delta_kernel(
    count,
    groups,
    q_ref,
    k_ref,
    v_ref,
    gate_ref,
    tail_ref,
    beta_ref,
    decay_ref,
    decay_t_ref,
    length_ref,
    cq_ref,
    ck_ref,
    cv_ref,
    rate_ref,
    rate_t_ref,
    gain_ref,
    w_ref,
    out_ref,
    full_ref,
    joined,
    enter,
    leave,
    send_sems,
    recv_sems,
    own_sem,
    z_send,
    z_recv,
    y_send,
    y_recv,
):
    me = lax.axis_index("seq")
    rows = q_ref.shape[0]
    key_heads = q_ref.shape[1] // DK
    value_heads = v_ref.shape[1] // DV
    share = value_heads // key_heads
    barrier = pltpu.get_barrier_semaphore()

    for peer in (lax.rem(me + 1, count), lax.rem(me + count - 1, count)):
        pl.semaphore_signal(barrier, inc=1, device_id={"seq": peer}, device_id_type=MESH)
    part = lax.axis_index("groups")
    for e in range(1, groups):
        pl.semaphore_signal(
            barrier,
            inc=1,
            device_id={"groups": lax.rem(part + e, groups)},
            device_id_type=MESH,
        )
    pl.semaphore_wait(barrier, 1 + groups)

    depth = w_ref.shape[0]
    piece = depth // groups

    def rows_of(block, which):
        return full_ref.at[pl.ds(pl.multiple_of(block * depth + which * piece, piece), piece)]

    def inside(block):
        return (block >= 0) & (block < count)

    def clamp(block):
        return jnp.clip(block, 0, count - 1)

    def along(d, j):
        sign = 1 if d == 0 else -1
        block = clamp(me - sign * j)
        source = w_ref.at[pl.ds(pl.multiple_of(part * piece, piece), piece)]
        return pltpu.make_async_remote_copy(
            src_ref=source if j == 0 else rows_of(block, part),
            dst_ref=rows_of(block, part),
            send_sem=z_send.at[d, j],
            recv_sem=z_recv.at[d, j],
            device_id={"seq": clamp(me + sign)},
            device_id_type=MESH,
        ), inside(me - sign * j) & inside(me + sign)

    def landing(d, j):
        sign = 1 if d == 0 else -1
        block = clamp(me - sign * (j + 1))
        return pltpu.make_async_remote_copy(
            src_ref=rows_of(block, part),
            dst_ref=rows_of(block, part),
            send_sem=z_send.at[d, j],
            recv_sem=z_recv.at[d, j],
            device_id={"seq": clamp(me + sign)},
            device_id_type=MESH,
        ), inside(me - sign * (j + 1))

    def across(e, d, j, which):
        sign = 1 if d == 0 else -1
        block = clamp(me - sign * (j + 1))
        return pltpu.make_async_remote_copy(
            src_ref=rows_of(block, which),
            dst_ref=rows_of(block, which),
            send_sem=y_send.at[e - 1, d, j],
            recv_sem=y_recv.at[e - 1, d, j],
            device_id={"groups": lax.rem(part + e, groups)},
            device_id_type=MESH,
        )

    def relay(j):
        for d in range(2):
            copy, here = landing(d, j)

            @pl.when(here)
            def _():
                copy.wait_recv()
                for e in range(1, groups):
                    across(e, d, j, part).start()

            if j + 1 < count - 1:
                onward, go = along(d, j + 1)
                pl.when(go)(onward.start)

    own = pltpu.make_async_copy(
        w_ref, full_ref.at[pl.ds(pl.multiple_of(me * depth, depth), depth)], own_sem
    )
    for d in range(2):
        first_copy, go = along(d, 0)
        pl.when(go)(first_copy.start)
    own.start()

    @pl.when(me == 0)
    def _():
        enter[...] = jnp.zeros_like(enter)

    q_width = key_heads * DK
    joined[:PAD] = tail_ref[...]
    joined[PAD:, :q_width] = q_ref[...].astype(jnp.float32)
    joined[PAD:, q_width : 2 * q_width] = k_ref[...].astype(jnp.float32)
    joined[PAD:, 2 * q_width :] = v_ref[...].astype(jnp.float32)

    def conv(base, taps, h):
        column = base + h * DK
        total = jnp.zeros((rows, DK), jnp.float32)
        for j in range(CONV):
            first = PAD - CONV + 1 + j
            total = total + taps[j : j + 1, h * DK : (h + 1) * DK] * joined[
                first : first + rows, column : column + DK
            ]
        return total * jax.nn.sigmoid(total)

    def unit(x):
        return x / jnp.sqrt(jnp.sum(x * x, -1, keepdims=True) + EPSILON)

    length = length_ref[0]
    start = me * rows
    at_row = start + lax.broadcasted_iota(jnp.int32, (rows, value_heads), 0)
    alive = (at_row < length).astype(jnp.float32)
    at_column = start + lax.broadcasted_iota(jnp.int32, (value_heads, rows), 1)
    alive_t = (at_column < length).astype(jnp.float32)

    def softplus(x):
        return jnp.maximum(x, 0.0) + jnp.log1p(jnp.exp(-jnp.abs(x)))

    beta = jax.nn.sigmoid(beta_ref[...]) * alive
    step = -rate_ref[...] * softplus(decay_ref[...]) * alive
    step_t = -rate_t_ref[...] * softplus(decay_t_ref[...]) * alive_t
    row = lax.broadcasted_iota(jnp.int32, (rows, rows), 0)
    column = lax.broadcasted_iota(jnp.int32, (rows, rows), 1)
    inclusive = row >= column
    run = mm(inclusive.astype(jnp.float32), step)
    run_t = mm(step_t, (row <= column).astype(jnp.float32))
    growth = jnp.exp(run)
    ending = jnp.exp(run[rows - 1 : rows] - run)
    eye = (row == column).astype(jnp.float32)

    queries, keyset, grams, mixes = [], [], [], []
    for g in range(key_heads):
        q = unit(conv(0, cq_ref, g)) * DK ** (-0.5)
        k = unit(conv(q_width, ck_ref, g))
        queries.append(q)
        keyset.append(k)
        grams.append(mm(k, k, ((1,), (1,))))
        mixes.append(mm(q, k, ((1,), (1,))))

    within, lower, inverse = [], [], []
    for h in range(value_heads):
        spread = run[:, h : h + 1] - run_t[h : h + 1, :]
        w = jnp.where(inclusive, jnp.exp(jnp.where(inclusive, spread, 0.0)), 0.0)
        within.append(w)
        low = jnp.where(row > column, beta[:, h : h + 1] * w * grams[h // share], 0.0)
        lower.append(low)
        pair = (row // 2 == column // 2) & (row > column)
        inverse.append(eye - jnp.where(pair, low, 0.0))
    size = 2
    while size < rows:
        off = (row // (2 * size) == column // (2 * size)) & (row // size > column // size)
        half = [mm(jnp.where(off, low, 0.0), x) for low, x in zip(lower, inverse)]
        inverse = [x - mm(x, y) for x, y in zip(inverse, half)]
        size *= 2

    local, carry, transition, injected = [], [], [], []
    for h in range(value_heads):
        k = keyset[h // share]
        v = conv(2 * q_width, cv_ref, h)
        b = beta[:, h : h + 1]
        w = mm(inverse[h], b * growth[:, h : h + 1] * k)
        u = mm(inverse[h], b * v)
        mix = mixes[h // share] * within[h]
        stop = ending[:, h : h + 1] * k
        local.append(mm(mix, u))
        carry.append(growth[:, h : h + 1] * queries[h // share] - mm(mix, w))
        transition.append(
            growth[rows - 1 : rows, h : h + 1] * eye - mm(stop, w, ((0,), (0,)))
        )
        injected.append(mm(stop, u, ((0,), (0,))))

    relay(0)
    copies = []
    for h in range(value_heads):
        copy = pltpu.make_async_remote_copy(
            src_ref=leave.at[h],
            dst_ref=enter.at[h],
            send_sem=send_sems.at[h],
            recv_sem=recv_sems.at[h],
            device_id={"seq": lax.rem(me + 1, count)},
            device_id_type=MESH,
        )
        copies.append(copy)

        @pl.when(me > 0)
        def _():
            copy.wait_recv()

        state = enter[h]
        leave[h] = mm(transition[h], state) + injected[h]
        o = local[h] + mm(carry[h], state)
        scaled = o * lax.rsqrt(jnp.mean(o * o, -1, keepdims=True) + EPSILON) * gain_ref[...]
        gate = gate_ref[:, h * DV : (h + 1) * DV].astype(jnp.float32)
        out_ref[:, h * DV : (h + 1) * DV] = (
            scaled * (gate * jax.nn.sigmoid(gate))
        ).astype(out_ref.dtype)

        @pl.when(me < count - 1)
        def _():
            copy.start()

    @pl.when(me < count - 1)
    def _():
        for copy in copies:
            copy.wait_send()

    for j in range(1, count - 1):
        relay(j)
    own.wait()
    for j in range(count - 1):
        for d in range(2):
            sent, go = along(d, j)
            pl.when(go)(sent.wait_send)
            _, here = landing(d, j)

            @pl.when(here)
            def _():
                for e in range(1, groups):
                    across(e, d, j, part).wait_send()
                    across(e, d, j, lax.rem(part + groups - e, groups)).wait_recv()


def delta(count, weights, q, k, v, gate, beta_logit, decay_logit, seq_length, cq, ck, cv, rate, gain):
    rows, value_heads = beta_logit.shape
    width = q.shape[1] + k.shape[1] + v.shape[1]
    rim = rows - CONV + 1
    groups = lax.axis_size("groups")
    tail = jnp.concatenate([q[rim:], k[rim:], v[rim:]], 1)
    tail = shifted(tail, "seq", 1).astype(jnp.float32)
    tail = jnp.concatenate([jnp.zeros((PAD - CONV + 1, width), jnp.float32), tail], 0)
    vmem = pl.BlockSpec(memory_space=pltpu.VMEM)
    smem = pl.BlockSpec(memory_space=pltpu.SMEM)
    return pl.pallas_call(
        functools.partial(delta_kernel, count, groups),
        out_shape=(
            jax.ShapeDtypeStruct(gate.shape, jnp.bfloat16),
            jax.ShapeDtypeStruct((count * weights.shape[0], weights.shape[1]), jnp.bfloat16),
        ),
        in_specs=[vmem] * 8 + [smem] + [vmem] * 7,
        out_specs=(vmem, pl.BlockSpec(memory_space=pl.ANY)),
        scratch_shapes=[
            pltpu.VMEM((rows + PAD, width), jnp.float32),
            pltpu.VMEM((value_heads, DK, DV), jnp.float32),
            pltpu.VMEM((value_heads, DK, DV), jnp.float32),
            pltpu.SemaphoreType.DMA((value_heads,)),
            pltpu.SemaphoreType.DMA((value_heads,)),
            pltpu.SemaphoreType.DMA,
            pltpu.SemaphoreType.DMA((2, count - 1)),
            pltpu.SemaphoreType.DMA((2, count - 1)),
            pltpu.SemaphoreType.DMA((groups - 1, 2, count - 1)),
            pltpu.SemaphoreType.DMA((groups - 1, 2, count - 1)),
        ],
        compiler_params=pltpu.CompilerParams(
            collective_id=0, has_side_effects=True, vmem_limit_bytes=32 * 2**20
        ),
        cost_estimate=pl.CostEstimate(
            flops=50_000_000_000, bytes_accessed=4_000_000, transcendentals=0
        ),
        name="delta_rule",
    )(
        q,
        k,
        v,
        gate,
        tail,
        beta_logit,
        decay_logit,
        decay_logit.T,
        seq_length,
        cq,
        ck,
        cv,
        rate[None, :],
        rate[:, None],
        gain[None, :],
        weights,
    )


def shifted(shard, axis, by):
    count = lax.axis_size(axis)
    pairs = [(i, i + by) for i in range(count) if 0 <= i + by < count]
    return lax.ppermute(shard, axis, pairs)


def rms_scaled(tensor, gain_vector):
    return tensor * lax.rsqrt(jnp.mean(tensor * tensor, -1, keepdims=True) + EPSILON) * gain_vector


def pick(key_value_weight, query_weight):
    attention_channel_id = lax.axis_index("head")
    query_head_rows = query_weight.shape[1] // (2 * HEAD_WIDTH)
    key_value_head = attention_channel_id * query_head_rows // (QUERY_HEADS // KEY_VALUE_HEADS)
    key_start = key_value_head * HEAD_WIDTH
    value_offset = (KEY_VALUE_HEADS + key_value_head) * HEAD_WIDTH
    return jnp.concatenate(
        [
            lax.dynamic_slice_in_dim(key_value_weight, key_start, HEAD_WIDTH, 1),
            lax.dynamic_slice_in_dim(key_value_weight, value_offset, HEAD_WIDTH, 1),
        ],
        1,
    )


def shards(
    residual,
    query_in,
    key_in,
    value_in,
    gating_in,
    beta_logit,
    decay_logit,
    seq_length,
    conv_query,
    conv_key,
    conv_value,
    decay_rate,
    norm_gain,
    out_weight,
    attn_gain,
    query_weight,
    key_value_weight,
):
    row_count = residual.shape[0]
    seq_rank = lax.axis_index("seq")
    positions = seq_rank * row_count + jnp.arange(row_count, dtype=jnp.int32)
    length_now = seq_length[0]
    weights = jnp.concatenate([query_weight, pick(key_value_weight, query_weight)], 1)
    gated, all_weights = delta(
        lax.axis_size("seq"),
        weights,
        query_in,
        key_in,
        value_in,
        gating_in,
        beta_logit,
        decay_logit,
        seq_length,
        conv_query,
        conv_key,
        conv_value,
        decay_rate,
        norm_gain,
    )
    summed = lax.psum(jnp.dot(gated, out_weight, preferred_element_type=jnp.float32), "head")
    hidden_out = (residual.astype(jnp.float32) + summed).astype(jnp.bfloat16)
    normalized = rms_scaled(hidden_out.astype(jnp.float32), attn_gain).astype(jnp.bfloat16)
    query_head_rows = query_weight.shape[1] // (2 * HEAD_WIDTH)
    projected = jnp.dot(normalized, all_weights, preferred_element_type=jnp.float32)
    query_proj = projected[:, : query_weight.shape[1]]
    kv_proj = projected[:, query_weight.shape[1] :]
    query_proj = query_proj.reshape(row_count, query_head_rows, 2, HEAD_WIDTH)
    queries_att = query_proj[:, :, 0].astype(jnp.bfloat16)
    gating_att = query_proj[:, :, 1]
    half_rows = row_count // 2
    blocks = (queries_att[:half_rows], queries_att[half_rows:])
    block_positions = (positions[:half_rows], positions[half_rows:])
    start_state = (
        jnp.full((query_head_rows, half_rows), NEGATIVE, jnp.float32),
        jnp.zeros((query_head_rows, half_rows), jnp.float32),
        jnp.zeros((query_head_rows, half_rows, HEAD_WIDTH), jnp.float32),
    )
    running = (start_state, start_state)
    offset = jnp.int32(0)
    both = lax.all_gather(kv_proj.astype(jnp.bfloat16), "seq", axis=0, tiled=True)
    key_piece = both[:, :HEAD_WIDTH]
    value_piece = both[:, HEAD_WIDTH:]
    key_positions = jnp.arange(key_piece.shape[0], dtype=jnp.int32)
    updated = []
    for block_index in range(2):
        block_queries = blocks[block_index]
        query_positions = block_positions[block_index]
        needed = jnp.logical_and(offset <= query_positions[-1], offset < length_now)

        def refresh(recurrent_state):
            peak, total, accum = recurrent_state
            scores = jnp.einsum(
                "qhd,kd->hqk", block_queries, key_piece, preferred_element_type=jnp.float32
            ) * HEAD_WIDTH ** (-0.5)
            visible = (key_positions[None, :] <= query_positions[:, None]) & (
                key_positions[None, :] < length_now
            )
            scores = jnp.where(visible[None], scores, NEGATIVE)
            new_peak = jnp.maximum(peak, jnp.max(scores, -1))
            weights = jnp.where(visible[None], jnp.exp(scores - new_peak[..., None]), 0.0)
            return (
                new_peak,
                jnp.sum(weights, -1),
                jnp.einsum(
                    "hqk,kd->hqd",
                    weights.astype(jnp.bfloat16),
                    value_piece,
                    preferred_element_type=jnp.float32,
                ),
            )

        updated.append(
            lax.cond(needed, refresh, lambda recurrent_state: recurrent_state, running[block_index])
        )
    finished = tuple(updated)
    results = [
        (recurrent_state[2] / recurrent_state[1][..., None]).transpose(1, 0, 2)
        for recurrent_state in finished
    ]
    attended = jnp.concatenate(results, 0)
    attention_out = (
        (attended * jax.nn.sigmoid(gating_att))
        .astype(jnp.bfloat16)
        .reshape(row_count, query_head_rows * HEAD_WIDTH)
    )
    return (hidden_out, attention_out)


def solution(mesh):
    placed = (
        P(("groups", "seq"), None),
        P(("groups", "seq"), "head"),
        P(("groups", "seq"), "head"),
        P(("groups", "seq"), "head"),
        P(("groups", "seq"), "head"),
        P(("groups", "seq"), "head"),
        P(("groups", "seq"), "head"),
        P("groups"),
        P(None, "head"),
        P(None, "head"),
        P(None, "head"),
        P("head"),
        P(),
        P("head", None),
        P(),
        P("seq", "head"),
        P("seq", None),
    )
    return jax.shard_map(
        shards,
        mesh=mesh,
        in_specs=placed,
        out_specs=(P(("groups", "seq"), None), P(("groups", "seq"), "head")),
        check_vma=False,
    )
```

profile of v0, /device:TPU:0, one launch (start us, length us, event | category | flops | bytes accessed | tf_op | source)
XLA Modules:
  0.0 230.6 jit_solution(18185394295972836157)
XLA Ops:
  7.3 0.9 slice.55
  8.2 0.7 slice.53
  8.9 0.7 slice.54
  9.6 0.6 pad_maximum_fusion.1
  10.2 5.5 %collective-permute-start = (bf16[3,2048]{1,0:T(4,128)(2,1)}, bf16[3,2048]{1,0:T(4,128)(2,1)}, u32[]{:S(2)}, u32[]{:S(2)}) collective-permute-start(bf16[3,2048]{1,0:T(4,128)(2,1)} %pad_maximum_fusion.1), channel_id=1, source_target_pairs={{0,4},{4,8},{8,12},{1,5},{5,9},{9,13},{2,6},{6,10},{10,14},{3,7},{... | collective-permute-start | bytes 36872 | tf_op jit(solution)/shard_map/ppermute | solution.py:349
  15.8 1.1 constant_dynamic-slice_fusion.1
  16.8 1.8 pad_maximum_fusion.w_ref
  19.6 0.7 pad_convert_fusion.tail_ref
  20.4 0.7 copy-done.7
  21.1 0.7 copy-done.8
  21.8 0.7 copy-done.9
  22.5 124.9 %delta_rule.1 = (bf16[128,1024]{1,0:T(8,128)(2,1)S(1)}, bf16[2048,2560]{1,0:T(8,128)(2,1)S(1)}) custom-call(bf16[128,512]{1,0:T(8,128)(2,1)S(1)} %copy-done.4, bf16[128,512]{1,0:T(8,128)(2,1)S(1)} %copy-done.5, bf16[128,1024]{1,0:T(8,128)(2,1)S(1)} %copy-done.3, bf16[128,1024]{1,0:T(8,128)(2,1)S(1)} %copy-done.6, f32[8,2048]{1,0:T(8,128)S(1)} %pad_convert_fusion.tail_ref, ...), custom_call_target="tpu_custom_call" | custom-call | flops 49999998976 | bytes 4000000 | tf_op jit(solution)/shard_map/delta_rule/pallas_call | solution.py:299
  147.4 4.0 %copy-done = bf16[2048,2560]{1,0:T(8,128)(2,1)} copy-done((bf16[2048,2560]{1,0:T(8,128)(2,1)}, bf16[2048,2560]{1,0:T(8,128)(2,1)S(1)}, u32[]{:S(2)}) %copy-start) | copy-done | bytes 10485784
  151.4 1.7 fusion.39
  153.1 0.6 fusion.38
  155.0 39.6 %all-reduce.3.cloned.1.call-done = f32[128,2048]{1,0:T(8,128)} async-done(((f32[128,2048]{1,0:T(8,128)}), f32[128,2048]{1,0:T(8,128)}) %all-reduce.3.cloned.1.call-update) | async-done | bytes 1048592 | tf_op jit(solution)/shard_map/psum | solution.py:411
  194.6 1.5 fusion.26
  196.1 5.7 %fusion.29 = f32[128,2560]{1,0:T(8,128)S(1)} fusion(bf16[2048,2560]{1,0:T(8,128)(2,1)} %copy-done, bf16[128,2048]{1,0:T(8,128)(2,1)S(1)} %get-tuple-element.75, f32[2048]{0:T(1024)S(1)} %copy-done.14, f32[128]{0:T(128)S(1)} %add_rsqrt_fusion), kind=kOutput, calls=%fused_computation.41 | convolution fusion | flops 1343225856 | bytes 12329472 | tf_op jit(solution)/shard_map/dot_general | solution.py:415
  202.0 0.3 copy.33
  202.6 15.5 %all_gather.3 = bf16[512,512]{1,0:T(8,128)(2,1)S(1)} all-gather(bf16[128,512]{1,0:T(8,128)(2,1)S(1)} %slice.78), channel_id=1, replica_groups=mesh['groups'=2,'seq'=4,'head'=4] {'seq'}, dimensions={0}, use_global_device_ids=true | all-gather | bytes 655360 | tf_op jit(solution)/shard_map/all_gather | solution.py:431
  218.1 1.7 conditional.2
  218.1 0.7 broadcast_compare_fusion
  218.8 0.3 fusion.35
  219.2 0.3 fusion.4
  219.5 0.2 fusion.3
  220.1 1.7 conditional.3
  220.1 0.7 broadcast_compare_fusion.1
  220.9 0.3 fusion.36
  221.3 0.3 fusion.17
  221.6 0.2 fusion.16
  222.7 0.2 fusion.31
  222.9 0.9 copy.40
  (55 shorter events, 2.2 us)
Async XLA Ops:
  7.2 13.1 %copy-start.3 = (bf16[128,1024]{1,0:T(8,128)(2,1)S(1)}, bf16[128,1024]{1,0:T(8,128)(2,1)}, u32[]{:S(2)}) copy-start(bf16[128,1024]{1,0:T(8,128)(2,1)} %v_ref.1) | copy-start | bytes 786436
  7.2 13.1 %copy-start.4 = (bf16[128,512]{1,0:T(8,128)(2,1)S(1)}, bf16[128,512]{1,0:T(8,128)(2,1)}, u32[]{:S(2)}) copy-start(bf16[128,512]{1,0:T(8,128)(2,1)} %q_ref.1) | copy-start | bytes 393220
  7.2 13.1 %copy-start.5 = (bf16[128,512]{1,0:T(8,128)(2,1)S(1)}, bf16[128,512]{1,0:T(8,128)(2,1)}, u32[]{:S(2)}) copy-start(bf16[128,512]{1,0:T(8,128)(2,1)} %k_ref.1) | copy-start | bytes 393220
  7.2 12.1 %copy-start.15 = (f32[128,8]{0,1:T(8,128)S(1)}, f32[128,8]{0,1:T(8,128)}, u32[]{:S(2)}) copy-start(f32[128,8]{0,1:T(8,128)} %param.26) | copy-start | bytes 12292
  7.2 12.2 %copy-start.1 = (f32[128,8]{0,1:T(8,128)S(1)}, f32[128,8]{0,1:T(8,128)}, u32[]{:S(2)}) copy-start(f32[128,8]{0,1:T(8,128)} %param.27) | copy-start | bytes 12292
  7.2 12.3 %copy-start.2 = (f32[8]{0:T(128)S(1)}, f32[8]{0:T(128)}, u32[]{:S(2)}) copy-start(f32[8]{0:T(128)} %param.32) | copy-start | bytes 100
  7.2 13.1 %copy-start.10 = (f32[128]{0:T(128)S(1)}, f32[128]{0:T(128)}, u32[]{:S(2)}) copy-start(f32[128]{0:T(128)} %param.33) | copy-start | bytes 1540
  7.2 13.1 %copy-start.6 = (bf16[128,1024]{1,0:T(8,128)(2,1)S(1)}, bf16[128,1024]{1,0:T(8,128)(2,1)}, u32[]{:S(2)}) copy-start(bf16[128,1024]{1,0:T(8,128)(2,1)} %gate_ref.1) | copy-start | bytes 786436
  7.2 187.4 %all-reduce.3.cloned.1.call-start = ((), (), s32[]{:S(2)}) async-start(), calls=%async_computation | async-start | bytes 2097152 | tf_op jit(solution)/shard_map/psum | solution.py:411
  10.2 9.4 %collective-permute-start = (bf16[3,2048]{1,0:T(4,128)(2,1)}, bf16[3,2048]{1,0:T(4,128)(2,1)}, u32[]{:S(2)}, u32[]{:S(2)}) collective-permute-start(bf16[3,2048]{1,0:T(4,128)(2,1)} %pad_maximum_fusion.1), channel_id=1, source_target_pairs={{0,4},{4,8},{8,12},{1,5},{5,9},{9,13},{2,6},{6,10},{10,14},{3,7},{... | collective-permute-start | bytes 36872 | tf_op jit(solution)/shard_map/ppermute | solution.py:349
  20.4 0.7 copy-start.7
  21.1 0.7 copy-start.8
  21.8 0.7 copy-start.9
  22.5 128.9 %copy-start.11 = (bf16[1024,2048]{1,0:T(8,128)(2,1)S(1)}, bf16[1024,2048]{1,0:T(8,128)(2,1)}, u32[]{:S(2)}) copy-start(bf16[1024,2048]{1,0:T(8,128)(2,1)} %param.34) | copy-start | bytes 12582916
  147.4 4.0 %copy-start = (bf16[2048,2560]{1,0:T(8,128)(2,1)}, bf16[2048,2560]{1,0:T(8,128)(2,1)S(1)}, u32[]{:S(2)}) copy-start(bf16[2048,2560]{1,0:T(8,128)(2,1)S(1)} %get-tuple-element.53) | copy-start | bytes 31457284
  151.4 43.3 %copy-start.13 = (bf16[128,2048]{1,0:T(8,128)(2,1)S(1)}, bf16[128,2048]{1,0:T(8,128)(2,1)}, u32[]{:S(2)}) copy-start(bf16[128,2048]{1,0:T(8,128)(2,1)} %param.21) | copy-start | bytes 1572868
  151.4 44.7 %copy-start.14 = (f32[2048]{0:T(1024)S(1)}, f32[2048]{0:T(1024)}, u32[]{:S(2)}) copy-start(f32[2048]{0:T(1024)} %param.35) | copy-start | bytes 24580
  196.1 5.8 %copy-start.12 = (bf16[128,2048]{1,0:T(8,128)(2,1)}, bf16[128,2048]{1,0:T(8,128)(2,1)S(1)}, u32[]{:S(2)}) copy-start(bf16[128,2048]{1,0:T(8,128)(2,1)S(1)} %get-tuple-element.75) | copy-start | bytes 1572868
Sparse Core Ops, SparseCore 0:
  153.2 41.3 all-reduce.2
where the time goes:
time: 231 us
  Pallas kernels  125 us (54%)
  waiting for transfers between devices  39.6 us (17%)
  between operations  16.3 us (7%)
  blocking collectives  15.5 us (7%)
  local copies, waits for them, and re-layouts  12.7 us (5%)
  matrix products  8.72 us (4%)
  other arithmetic  7.15 us (3%)
  starting transfers between devices  5.58 us (2%)
    pallas_call x1, Pallas kernels, delta(): pl.pallas_call(functools.partial(delta_kernel, count, groups), out_shape=...  125 us
    psum x1, waiting for transfers between devices, shards(): lax.psum(jnp.dot(gated, out_weight, preferred_element_type=jnp.float32),...  39.6 us
    all_gather x1, blocking collectives, shards(): lax.all_gather(kv_proj.astype(jnp.bfloat16), 'seq', axis=0, tiled=True)  15.5 us
    unnamed x36, local copies, waits for them, and re-layouts  7.38 us
    dot_general x1, matrix products, shards(): jnp.dot(normalized, all_weights, preferred_element_type=jnp.float32)  5.75 us
    ppermute x1, starting transfers between devices, shifted(): return lax.ppermute(shard, axis, pairs)  5.54 us
  transfers between devices with their start and end apart: 2, of which 1 were waited for; matrix products, arithmetic and copies ran while one was open for 2% of the time, Pallas kernels for 0%

commit v1 on v0

v1 whole, which is shorter than its diff:
```python
import functools

import jax
import jax.numpy as jnp
from jax import lax
from jax.experimental import pallas as pl
from jax.experimental.pallas import tpu as pltpu
from jax.sharding import PartitionSpec as P

DK = 128
DV = 128
QUERY_HEADS = 16
KEY_VALUE_HEADS = 2
HEAD_WIDTH = 256
CONV = 4
PAD = 8
TAIL = 16
MATES = 2
EARLY = 3

EPSILON = 1e-06
NEGATIVE = -1e30
MESH = pl.DeviceIdType.MESH
HIGHEST = lax.Precision.HIGHEST


def exact(a, b, contract=((1,), (0,))):
    return lax.dot_general(
        a, b, (contract, ((), ())), precision=HIGHEST, preferred_element_type=jnp.float32
    )


def mm(a, b, contract=((1,), (0,))):
    return lax.dot_general(
        a.astype(jnp.bfloat16),
        b.astype(jnp.bfloat16),
        (contract, ((), ())),
        preferred_element_type=jnp.float32,
    )


def softplus(x):
    return jnp.maximum(x, 0.0) + jnp.log1p(jnp.exp(-jnp.abs(x)))


def unit(x):
    return x / jnp.sqrt(jnp.sum(x * x, -1, keepdims=True) + EPSILON)


def kernel(
    count,
    groups,
    heads,
    residual_in,
    q_in,
    k_in,
    v_in,
    gate_in,
    beta_in,
    decay_in,
    length_ref,
    cq_in,
    ck_in,
    cv_in,
    rate_in,
    gain_in,
    ow_in,
    again_in,
    qw_in,
    kvw_in,
    hidden_out,
    attention_out,
    q_ref,
    k_ref,
    v_ref,
    gate_ref,
    beta_ref,
    decay_ref,
    cq_ref,
    ck_ref,
    cv_ref,
    rate_ref,
    gain_ref,
    ow_ref,
    again_ref,
    residual_ref,
    wq,
    wkv,
    tail_q,
    tail_k,
    tail_v,
    joined,
    mapping,
    local,
    injected,
    enter,
    leave,
    gated,
    summed,
    partial,
    landed,
    hidden,
    normed,
    kvall,
    attended,
    load_sems,
    tail_send,
    tail_recv,
    state_send,
    state_recv,
    z_send,
    z_recv,
    y_send,
    y_recv,
    m_send,
    m_recv,
    my_send,
    my_recv,
    rs_send,
    rs_recv,
    ag_send,
    ag_recv,
    kv_send,
    kv_recv,
    km_send,
    km_recv,
):
    me = lax.axis_index("seq")
    part = lax.axis_index("groups")
    lane = lax.axis_index("head")
    core = lax.rem(lane, MATES)
    mate = lane + 1 - 2 * core
    rows = q_ref.shape[0]
    key_heads = q_ref.shape[1] // DK
    value_heads = v_ref.shape[1] // DV
    share = value_heads // key_heads
    query_heads = wq.shape[0]
    units = query_heads + 1
    depth = qw_in.shape[0]
    piece = depth // groups
    quarter = piece // MATES
    slab = rows // heads
    early = min(EARLY, units)
    kv_head = lane * query_heads // (QUERY_HEADS // KEY_VALUE_HEADS)

    loads = []

    def load(source, target):
        copy = pltpu.make_async_copy(source, target, load_sems.at[len(loads)])
        copy.start()
        loads.append(copy)
        return copy

    own_rows = pl.ds(pl.multiple_of(me * depth, depth), depth)
    load_kv = [
        load(
            kvw_in.at[
                :, pl.ds(pl.multiple_of((kind * KEY_VALUE_HEADS + kv_head) * HEAD_WIDTH, HEAD_WIDTH), HEAD_WIDTH)
            ],
            wkv.at[own_rows, pl.ds(kind * HEAD_WIDTH, HEAD_WIDTH)],
        )
        for kind in range(2)
    ]
    load_decay = [load(a, b) for a, b in ((decay_in, decay_ref), (rate_in, rate_ref), (beta_in, beta_ref))]
    load_conv = [
        load(a, b)
        for a, b in (
            (q_in, q_ref),
            (k_in, k_ref),
            (v_in, v_ref),
            (cq_in, cq_ref),
            (ck_in, ck_ref),
            (cv_in, cv_ref),
        )
    ]

    barrier = pltpu.get_barrier_semaphore()
    for axis, size, place in (("seq", count, me), ("groups", groups, part), ("head", heads, lane)):
        for e in range(1, size):
            pl.semaphore_signal(
                barrier, inc=1, device_id={axis: lax.rem(place + e, size)}, device_id_type=MESH
            )
    pl.semaphore_wait(barrier, count + groups + heads - 3)

    def inside(block):
        return (block >= 0) & (block < count)

    def clamp(block):
        return jnp.clip(block, 0, count - 1)

    def remote(source, target, send, recv, axis, index):
        return pltpu.make_async_remote_copy(
            src_ref=source,
            dst_ref=target,
            send_sem=send,
            recv_sem=recv,
            device_id={axis: index},
            device_id_type=MESH,
        )

    follower = clamp(me + 1)
    tails = [
        remote(
            source.at[pl.ds(rows - TAIL, TAIL)],
            target,
            tail_send.at[i],
            tail_recv.at[i],
            "seq",
            follower,
        )
        for i, (source, target) in enumerate(((q_in, tail_q), (k_in, tail_k), (v_in, tail_v)))
    ]

    @pl.when(me < count - 1)
    def _():
        for copy in tails:
            copy.start()

    def spot(block, which, half, u):
        if u == 0:
            first = block * depth + which * piece + half * quarter
            return wkv.at[pl.ds(pl.multiple_of(first, quarter), quarter)]
        first = block * depth + which * piece
        return wq.at[u - 1, pl.ds(pl.multiple_of(first, piece), piece)]

    def sign_of(d):
        return 1 if d == 0 else -1

    def along(d, j, u):
        sign = sign_of(d)
        block = clamp(me - sign * j)
        target = spot(block, part, core, u)
        source = target
        if j == 0 and u > 0:
            source = qw_in.at[
                pl.ds(pl.multiple_of(part * piece, piece), piece),
                pl.ds((u - 1) * 2 * HEAD_WIDTH, 2 * HEAD_WIDTH),
            ]
        copy = remote(
            source, target, z_send.at[d, j, u], z_recv.at[d, j, u], "seq", clamp(me + sign)
        )
        return copy, inside(me - sign * j) & inside(me + sign)

    def arriving(d, j, u):
        sign = sign_of(d)
        target = spot(clamp(me - sign * (j + 1)), part, core, u)
        copy = remote(
            target, target, z_send.at[d, j, u], z_recv.at[d, j, u], "seq", clamp(me + sign)
        )
        return copy, inside(me - sign * (j + 1))

    def across(e, d, j, u, which):
        target = spot(clamp(me - sign_of(d) * (j + 1)), which, core, u)
        return remote(
            target,
            target,
            y_send.at[e - 1, d, j, u],
            y_recv.at[e - 1, d, j, u],
            "groups",
            lax.rem(part + e, groups),
        )

    def beside(d, j, half):
        target = spot(clamp(me - sign_of(d) * (j + 1)), part, half, 0)
        return remote(target, target, m_send.at[d, j], m_recv.at[d, j], "head", mate)

    def source_of(e):
        return lax.rem(part + groups - e, groups)

    def beyond(e, d, j, half):
        target = spot(clamp(me - sign_of(d) * (j + 1)), source_of(e), half, 0)
        return remote(
            target, target, my_send.at[e - 1, d, j], my_recv.at[e - 1, d, j], "head", mate
        )

    def onward(d, j, u):
        if j + 1 < count - 1:
            copy, go = along(d, j + 1, u)
            pl.when(go)(copy.start)

    def relay(d, j, u, forward=True):
        copy, here = arriving(d, j, u)

        @pl.when(here)
        def _():
            copy.wait_recv()
            for e in range(1, groups):
                across(e, d, j, u, part).start()
            if u == 0:
                beside(d, j, core).start()

        if forward:
            onward(d, j, u)

    def share_kv(d, j):
        _, here = arriving(d, j, 0)

        @pl.when(here)
        def _():
            for e in range(1, groups):
                across(e, d, j, 0, source_of(e)).wait_recv()
                beyond(e, d, j, core).start()

    for copy in load_kv:
        copy.wait()
    for u in range(units):
        for d in range(2):
            if d == 1 or u < early:
                copy, go = along(d, 0, u)
                pl.when(go)(copy.start)

    load_late = [
        load(gate_in, gate_ref),
        load(gain_in, gain_ref),
        load(ow_in, ow_ref),
        load(residual_in.at[pl.ds(pl.multiple_of(lane * slab, slab), slab)], residual_ref),
        load(again_in, again_ref),
    ]
    load_q = [
        load(qw_in.at[:, pl.ds(i * 2 * HEAD_WIDTH, 2 * HEAD_WIDTH)], wq.at[i, own_rows])
        for i in range(query_heads)
    ]

    for b in range(1, count):

        @pl.when(b > me)
        def _():
            kvall[:, b * rows : (b + 1) * rows] = jnp.zeros((2, rows, HEAD_WIDTH), kvall.dtype)

    for copy in load_decay:
        copy.wait()
    length = length_ref[0]
    at_row = me * rows + lax.broadcasted_iota(jnp.int32, (rows, value_heads), 0)
    alive = (at_row < length).astype(jnp.float32)
    beta = jax.nn.sigmoid(beta_ref[...]) * alive
    step = -rate_ref[...] * softplus(decay_ref[...]) * alive
    row = lax.broadcasted_iota(jnp.int32, (rows, rows), 0)
    column = lax.broadcasted_iota(jnp.int32, (rows, rows), 1)
    inclusive = row >= column
    run = exact(inclusive.astype(jnp.float32), step)
    run_t = exact(step, (row <= column).astype(jnp.float32), ((0,), (0,)))
    growth = jnp.exp(run)
    ending_t = jnp.exp(run_t[:, rows - 1 : rows] - run_t)
    eye = (row == column).astype(jnp.float32)

    for copy in load_conv:
        copy.wait()
    q_width = key_heads * DK
    joined[PAD:, :q_width] = q_ref[...].astype(jnp.float32)
    joined[PAD:, q_width : 2 * q_width] = k_ref[...].astype(jnp.float32)
    joined[PAD:, 2 * q_width :] = v_ref[...].astype(jnp.float32)

    @pl.when(me == 0)
    def _():
        enter[...] = jnp.zeros_like(enter)
        joined[:PAD] = jnp.zeros((PAD, joined.shape[1]), jnp.float32)

    @pl.when(me > 0)
    def _():
        for copy in tails:
            copy.wait_recv()
        joined[:PAD, :q_width] = tail_q[...].astype(jnp.float32)[TAIL - PAD :]
        joined[:PAD, q_width : 2 * q_width] = tail_k[...].astype(jnp.float32)[TAIL - PAD :]
        joined[:PAD, 2 * q_width :] = tail_v[...].astype(jnp.float32)[TAIL - PAD :]

    def conv(base, taps, h):
        first_column = base + h * DK
        total = jnp.zeros((rows, DK), jnp.float32)
        for j in range(CONV):
            first = PAD - CONV + 1 + j
            total = total + taps[j : j + 1, h * DK : (h + 1) * DK] * joined[
                first : first + rows, first_column : first_column + DK
            ]
        return total * jax.nn.sigmoid(total)

    queries, keyset, turned, grams = [], [], [], []
    for g in range(key_heads):
        q = unit(conv(0, cq_ref, g)) * DK ** (-0.5)
        k = unit(conv(q_width, ck_ref, g))
        k_t = k.T
        queries.append(q)
        keyset.append(k)
        turned.append(k_t)
        grams.append(mm(jnp.concatenate([k, q], 0), k_t))

    for d in range(2):
        relay(d, 0, 0, forward=d == 1)

    mixes, lower, inverse = [], [], []
    for h in range(value_heads):
        spread = run[:, h : h + 1] - run_t[h : h + 1, :]
        w = jnp.exp(jnp.where(inclusive, spread, NEGATIVE))
        gram = grams[h // share]
        mixes.append((gram[rows:] * w).astype(jnp.bfloat16))
        low = jnp.where(row > column, beta[:, h : h + 1] * w * gram[:rows], 0.0)
        lower.append(low)
        pair = (row // 2 == column // 2) & (row > column)
        inverse.append(eye - jnp.where(pair, low, 0.0))
    size = 2
    while size < rows:
        off = (row // (2 * size) == column // (2 * size)) & (row // size > column // size)
        half = [mm(jnp.where(off, low, 0.0), x) for low, x in zip(lower, inverse)]
        inverse = [x - mm(x, y) for x, y in zip(inverse, half)]
        size *= 2
    if early > 1:
        for d in range(2):
            relay(d, 0, 1, forward=d == 1)

    for h in range(value_heads):
        k = keyset[h // share]
        v = conv(2 * q_width, cv_ref, h)
        b = beta[:, h : h + 1]
        grown = growth[:, h : h + 1]
        wu = mm(inverse[h], jnp.concatenate([b * grown * k, b * v], 1))
        stop_t = (turned[h // share] * ending_t[h : h + 1, :]).astype(jnp.bfloat16)
        both = mm(jnp.concatenate([stop_t, mixes[h]], 0), wu)
        mapping[h, :DK] = both[:DK, :DK].astype(jnp.bfloat16)
        mapping[h, DK:] = (grown * queries[h // share] - both[DK:, :DK]).astype(jnp.bfloat16)
        injected[h] = both[:DK, DK:]
        local[h] = both[DK:, DK:]
    if early > 2:
        for d in range(2):
            relay(d, 0, 2, forward=d == 1)

    for copy in load_late[:2]:
        copy.wait()
    states = []
    for h in range(value_heads):
        copy = remote(
            leave.at[h], enter.at[h], state_send.at[h], state_recv.at[h], "seq", follower
        )
        states.append(copy)

        @pl.when(me > 0)
        def _():
            copy.wait_recv()

        state = enter[h]
        moved = mm(mapping[h], state)
        total = growth[rows - 1 : rows, h : h + 1] * state.astype(jnp.float32)
        leave[h] = (total - moved[:DK] + injected[h]).astype(leave.dtype)
        o = local[h] + moved[DK:]
        scaled = o * lax.rsqrt(jnp.mean(o * o, -1, keepdims=True) + EPSILON) * gain_ref[...]
        gate = gate_ref[:, h * DV : (h + 1) * DV].astype(jnp.float32)
        gated[:, h * DV : (h + 1) * DV] = (scaled * (gate * jax.nn.sigmoid(gate))).astype(
            gated.dtype
        )

        @pl.when(me < count - 1)
        def _():
            copy.start()

    for u in range(early, units):
        copy, go = along(0, 0, u)
        pl.when(go)(copy.start)
    for u in range(early):
        onward(0, 0, u)

    for copy in load_late[2:]:
        copy.wait()
    width = ow_ref.shape[1]
    tile = min(512, width)
    for c in range(0, width, tile):
        product = jnp.dot(
            gated[...], ow_ref[:, c : c + tile], preferred_element_type=jnp.float32
        )
        summed[:, c : c + tile] = product
        partial[:, c : c + tile] = product.astype(partial.dtype)

    def slab_of(index):
        return pl.ds(pl.multiple_of(index * slab, slab), slab)

    scatter, gather = [], []
    for e in range(1, heads):
        peer = lax.rem(lane + e, heads)
        scatter.append(
            remote(
                partial.at[slab_of(peer)],
                landed.at[e - 1],
                rs_send.at[e - 1],
                rs_recv.at[e - 1],
                "head",
                peer,
            )
        )
        gather.append(
            remote(
                hidden.at[slab_of(lane)],
                hidden.at[slab_of(lane)],
                ag_send.at[e - 1],
                ag_recv.at[e - 1],
                "head",
                peer,
            )
        )
    for copy in scatter:
        copy.start()
    for u in range(early, units):
        for d in range(2):
            relay(d, 0, u)
    for d in range(2):
        share_kv(d, 0)
    for copy in scatter:
        copy.wait_recv()
    total = residual_ref[...].astype(jnp.float32) + (
        summed[slab_of(lane)] + sum(landed[e].astype(jnp.float32) for e in range(heads - 1))
    )
    hidden[slab_of(lane)] = total.astype(hidden.dtype)
    for copy in gather:
        copy.start()
    for j in range(1, count - 1):
        for d in range(2):
            relay(d, j, 0)
    for j in range(1, count - 1):
        for d in range(2):
            share_kv(d, j)
    for e in range(1, heads):
        peer = lax.rem(lane + heads - e, heads)
        remote(
            hidden.at[slab_of(peer)],
            hidden.at[slab_of(peer)],
            ag_send.at[e - 1],
            ag_recv.at[e - 1],
            "head",
            peer,
        ).wait_recv()
    save_hidden = load(hidden, hidden_out)
    widened = hidden[...].astype(jnp.float32)
    normed[...] = (
        widened
        * lax.rsqrt(jnp.mean(widened * widened, -1, keepdims=True) + EPSILON)
        * again_ref[...]
    ).astype(normed.dtype)

    for j in range(count - 1):
        for d in range(2):
            _, here = arriving(d, j, 0)

            @pl.when(here)
            def _():
                beside(d, j, 1 - core).wait_recv()
                for e in range(1, groups):
                    beyond(e, d, j, 1 - core).wait_recv()

    own_block = pl.ds(pl.multiple_of(me * rows, rows), rows)
    for kind in range(2):
        kvall[kind, own_block] = jnp.dot(
            normed[...],
            wkv[:, kind * HEAD_WIDTH : (kind + 1) * HEAD_WIDTH],
            preferred_element_type=jnp.float32,
        ).astype(kvall.dtype)

    def block_at(block):
        return pl.ds(pl.multiple_of(clamp(block) * rows, rows), rows)

    def later(e, block, axis, index, kind, send, recv):
        place = kvall.at[kind, block_at(block)]
        return remote(place, place, send.at[e - 1], recv.at[e - 1], axis, index)

    for e in range(1, count):

        @pl.when(me + e < count)
        def _():
            later(e, me, "seq", clamp(me + e), core, kv_send, kv_recv).start()

    for j in range(1, count - 1):
        for u in range(1, units):
            for d in range(2):
                if (j, u) < (count - 2, 1) or count == 2:
                    relay(d, j, u)

    for e in range(1, count):

        @pl.when(me >= e)
        def _():
            later(e, me - e, "seq", clamp(me - e), core, kv_send, kv_recv).wait_recv()
            later(e, me - e, "head", mate, core, km_send, km_recv).start()

    for e in range(1, count):

        @pl.when(me >= e)
        def _():
            later(e, me - e, "head", mate, 1 - core, km_send, km_recv).wait_recv()

    for copy in load_q:
        copy.wait()
    keys_total = count * rows
    at_query = me * rows + lax.broadcasted_iota(jnp.int32, (rows, keys_total), 0)
    at_key = lax.broadcasted_iota(jnp.int32, (rows, keys_total), 1)
    visible = (at_key <= at_query) & (at_key < length)
    for i in range(query_heads):
        if count > 2:
            for d in range(2):
                relay(d, count - 2, i + 1)
        for j in range(count - 1):
            for d in range(2):
                _, here = arriving(d, j, i + 1)

                @pl.when(here)
                def _():
                    for e in range(1, groups):
                        across(e, d, j, i + 1, source_of(e)).wait_recv()

        projected = jnp.dot(normed[...], wq[i], preferred_element_type=jnp.float32)
        scores = (
            lax.dot_general(
                projected[:, :HEAD_WIDTH].astype(jnp.bfloat16),
                kvall[0],
                (((1,), (1,)), ((), ())),
                preferred_element_type=jnp.float32,
            )
            * HEAD_WIDTH ** (-0.5)
        )
        scores = jnp.where(visible, scores, NEGATIVE)
        peak = jnp.max(scores, -1, keepdims=True)
        weights = jnp.where(visible, jnp.exp(scores - peak), 0.0)
        norm = jnp.sum(weights, -1, keepdims=True)
        mixed = jnp.dot(
            weights.astype(jnp.bfloat16), kvall[1], preferred_element_type=jnp.float32
        )
        attended[:, i * HEAD_WIDTH : (i + 1) * HEAD_WIDTH] = (
            mixed / norm * jax.nn.sigmoid(projected[:, HEAD_WIDTH:])
        ).astype(attended.dtype)
    save_attended = load(attended, attention_out)

    @pl.when(me < count - 1)
    def _():
        for copy in tails + states:
            copy.wait_send()

    for copy in scatter + gather:
        copy.wait_send()
    for j in range(count - 1):
        for d in range(2):
            for u in range(units):
                copy, go = along(d, j, u)
                pl.when(go)(copy.wait_send)
            _, here = arriving(d, j, 0)

            @pl.when(here)
            def _():
                for e in range(1, groups):
                    for u in range(units):
                        across(e, d, j, u, part).wait_send()
                    beyond(e, d, j, core).wait_send()
                beside(d, j, core).wait_send()

    for e in range(1, count):

        @pl.when(me + e < count)
        def _():
            later(e, me, "seq", clamp(me + e), core, kv_send, kv_recv).wait_send()

        @pl.when(me >= e)
        def _():
            later(e, me - e, "head", mate, core, km_send, km_recv).wait_send()

    save_hidden.wait()
    save_attended.wait()


def shards(
    residual,
    query_in,
    key_in,
    value_in,
    gating_in,
    beta_logit,
    decay_logit,
    seq_length,
    conv_query,
    conv_key,
    conv_value,
    decay_rate,
    norm_gain,
    out_weight,
    attn_gain,
    query_weight,
    key_value_weight,
):
    count = lax.axis_size("seq")
    groups = lax.axis_size("groups")
    heads = lax.axis_size("head")
    rows, model = residual.shape
    value_heads = beta_logit.shape[1]
    query_heads = query_weight.shape[1] // (2 * HEAD_WIDTH)
    units = query_heads + 1
    width = query_in.shape[1] + key_in.shape[1] + value_in.shape[1]
    depth = query_weight.shape[0] * count
    f32, bf16 = jnp.float32, jnp.bfloat16
    dma = pltpu.SemaphoreType.DMA
    anywhere = pl.BlockSpec(memory_space=pl.ANY)
    smem = pl.BlockSpec(memory_space=pltpu.SMEM)
    rate = decay_rate[None, :]
    gain = norm_gain[None, :]
    attn = attn_gain[None, :]
    like = lambda a: pltpu.VMEM(a.shape, a.dtype)
    return pl.pallas_call(
        functools.partial(kernel, count, groups, heads),
        out_shape=(
            jax.ShapeDtypeStruct(residual.shape, bf16),
            jax.ShapeDtypeStruct((rows, query_heads * HEAD_WIDTH), bf16),
        ),
        in_specs=[anywhere] * 7 + [smem] + [anywhere] * 9,
        out_specs=(anywhere, anywhere),
        scratch_shapes=[
            like(query_in),
            like(key_in),
            like(value_in),
            like(gating_in),
            like(beta_logit),
            like(decay_logit),
            like(conv_query),
            like(conv_key),
            like(conv_value),
            like(rate),
            like(gain),
            like(out_weight),
            like(attn),
            pltpu.VMEM((rows // heads, model), bf16),
            pltpu.VMEM((query_heads, depth, 2 * HEAD_WIDTH), bf16),
            pltpu.VMEM((depth, 2 * HEAD_WIDTH), bf16),
            pltpu.VMEM((TAIL, query_in.shape[1]), bf16),
            pltpu.VMEM((TAIL, key_in.shape[1]), bf16),
            pltpu.VMEM((TAIL, value_in.shape[1]), bf16),
            pltpu.VMEM((rows + PAD, width), f32),
            pltpu.VMEM((value_heads, DK + rows, DK), bf16),
            pltpu.VMEM((value_heads, rows, DV), f32),
            pltpu.VMEM((value_heads, DK, DV), f32),
            pltpu.VMEM((value_heads, DK, DV), bf16),
            pltpu.VMEM((value_heads, DK, DV), bf16),
            pltpu.VMEM((rows, value_heads * DV), bf16),
            pltpu.VMEM((rows, model), f32),
            pltpu.VMEM((rows, model), bf16),
            pltpu.VMEM((heads - 1, rows // heads, model), bf16),
            pltpu.VMEM((rows, model), bf16),
            pltpu.VMEM((rows, model), bf16),
            pltpu.VMEM((2, count * rows, HEAD_WIDTH), bf16),
            pltpu.VMEM((rows, query_heads * HEAD_WIDTH), bf16),
            dma((24 + query_heads,)),
            dma((3,)),
            dma((3,)),
            dma((value_heads,)),
            dma((value_heads,)),
            dma((2, count - 1, units)),
            dma((2, count - 1, units)),
            dma((groups - 1, 2, count - 1, units)),
            dma((groups - 1, 2, count - 1, units)),
            dma((2, count - 1)),
            dma((2, count - 1)),
            dma((groups - 1, 2, count - 1)),
            dma((groups - 1, 2, count - 1)),
            dma((heads - 1,)),
            dma((heads - 1,)),
            dma((heads - 1,)),
            dma((heads - 1,)),
            dma((count - 1,)),
            dma((count - 1,)),
            dma((count - 1,)),
            dma((count - 1,)),
        ],
        compiler_params=pltpu.CompilerParams(
            collective_id=0, has_side_effects=True, vmem_limit_bytes=56 * 2**20
        ),
        name="layer",
    )(
        residual,
        query_in,
        key_in,
        value_in,
        gating_in,
        beta_logit,
        decay_logit,
        seq_length,
        conv_query,
        conv_key,
        conv_value,
        rate,
        gain,
        out_weight,
        attn,
        query_weight,
        key_value_weight,
    )


def solution(mesh):
    placed = (
        P(("groups", "seq"), None),
        P(("groups", "seq"), "head"),
        P(("groups", "seq"), "head"),
        P(("groups", "seq"), "head"),
        P(("groups", "seq"), "head"),
        P(("groups", "seq"), "head"),
        P(("groups", "seq"), "head"),
        P("groups"),
        P(None, "head"),
        P(None, "head"),
        P(None, "head"),
        P("head"),
        P(),
        P("head", None),
        P(),
        P("seq", "head"),
        P("seq", None),
    )
    return jax.shard_map(
        shards,
        mesh=mesh,
        in_specs=placed,
        out_specs=(P(("groups", "seq"), None), P(("groups", "seq"), "head")),
        check_vma=False,
    )
```

time: 231 us -> 146 us (0.63)
  the two profiles are of different devices: /device:TPU:0 before, /device:TPU:24 now
where the time goes in v1:
time: 146 us
  Pallas kernels  138 us (95%)
  local copies, waits for them, and re-layouts  6.38 us (4%)
    pallas_call x1, Pallas kernels, shards(): pl.pallas_call(functools.partial(kernel, count, groups, heads), out_shape...  138 us
    unnamed x4, local copies, waits for them, and re-layouts  6.38 us

profile of v1, /device:TPU:24, one launch (start us, length us, event | category | flops | bytes accessed | tf_op | source)
XLA Modules:
  0.0 146.1 jit_solution(5557899657206329731)
XLA Ops:
  1.3 1.4 copy.19.beta_in
  2.7 1.4 copy.20.decay_in
  4.1 138.4 %layer.1 = (bf16[128,2048]{1,0:T(8,128)(2,1)}, bf16[128,1024]{1,0:T(8,128)(2,1)}) custom-call(bf16[128,2048]{1,0:T(8,128)(2,1)} %residual_in.1, bf16[128,512]{1,0:T(8,128)(2,1)} %q_in.1, bf16[128,512]{1,0:T(8,128)(2,1)} %k_in.1, bf16[128,1024]{1,0:T(8,128)(2,1)} %v_in.1, bf16[128,1024]{1,0:T(8,128)(2,1)} %gate_in.1, f32[128,8]{1,0:T(8,128)} %copy.19.beta_in, ...), custom_call_target="tpu_custom_call" | custom-call | tf_op jit(solution)/shard_map/layer/pallas_call | solution.py:698
  142.6 1.9 %copy.24 = bf16[128,2048]{1,0:T(8,128)(2,1)} copy(bf16[128,2048]{1,0:T(8,128)(2,1)} %get-tuple-element.4) | data formatting | bytes 1048576
  144.4 1.7 %copy.25 = bf16[128,1024]{1,0:T(8,128)(2,1)} copy(bf16[128,1024]{1,0:T(8,128)(2,1)} %get-tuple-element.5) | data formatting | bytes 524288

commit v2 on v0

v2 whole, which is shorter than its diff:
```python
import functools

import jax
import jax.numpy as jnp
from jax import lax
from jax.experimental import pallas as pl
from jax.experimental.pallas import tpu as pltpu
from jax.sharding import PartitionSpec as P

DK = 128
DV = 128
QUERY_HEADS = 16
KEY_VALUE_HEADS = 2
HEAD_WIDTH = 256
CONV = 4
PAD = 8
TAIL = 16
MATES = 2
EARLY = 3

EPSILON = 1e-06
NEGATIVE = -1e30
MESH = pl.DeviceIdType.MESH
HIGHEST = lax.Precision.HIGHEST


def exact(a, b, contract=((1,), (0,))):
    return lax.dot_general(
        a, b, (contract, ((), ())), precision=HIGHEST, preferred_element_type=jnp.float32
    )


def mm(a, b, contract=((1,), (0,))):
    return lax.dot_general(
        a.astype(jnp.bfloat16),
        b.astype(jnp.bfloat16),
        (contract, ((), ())),
        preferred_element_type=jnp.float32,
    )


def softplus(x):
    return jnp.maximum(x, 0.0) + jnp.log1p(jnp.exp(-jnp.abs(x)))


def unit(x):
    return x / jnp.sqrt(jnp.sum(x * x, -1, keepdims=True) + EPSILON)


INPUTS = [
    "residual_in",
    "q_in",
    "k_in",
    "v_in",
    "gate_in",
    "beta_in",
    "decay_in",
    "length_ref",
    "cq_in",
    "ck_in",
    "cv_in",
    "rate_in",
    "gain_in",
    "ow_in",
    "again_in",
    "qw_in",
    "kvw_in",
]
OUTPUTS = ["hidden_out", "attention_out"]


def remote(source, target, send, recv, axis, index):
    return pltpu.make_async_remote_copy(
        src_ref=source,
        dst_ref=target,
        send_sem=send,
        recv_sem=recv,
        device_id={axis: index},
        device_id_type=MESH,
    )


def sign_of(d):
    return 1 if d == 0 else -1


class Layer:
    def __init__(self, sizes, names, refs):
        self.count, self.groups, self.heads = sizes
        for name, ref in zip(names, refs, strict=True):
            setattr(self, name, ref)
        self.me = lax.axis_index("seq")
        self.part = lax.axis_index("groups")
        self.lane = lax.axis_index("head")
        self.core = lax.rem(self.lane, MATES)
        self.mate = self.lane + 1 - 2 * self.core
        self.rows = self.q_ref.shape[0]
        self.key_heads = self.q_ref.shape[1] // DK
        self.value_heads = self.v_ref.shape[1] // DV
        self.share = self.value_heads // self.key_heads
        self.depth = self.qw_in.shape[0]
        self.piece = self.depth // self.groups
        self.quarter = self.piece // MATES
        self.slab = self.rows // self.heads
        self.query_heads = self.qw_in.shape[1] // (2 * HEAD_WIDTH)
        self.kv_head = self.lane * self.query_heads // (QUERY_HEADS // KEY_VALUE_HEADS)
        self.own_rows = pl.ds(pl.multiple_of(self.me * self.depth, self.depth), self.depth)
        self.follower = self.clamp(self.me + 1)
        self.loads = 0

    def load(self, source, target):
        copy = pltpu.make_async_copy(source, target, self.load_sems.at[self.loads])
        copy.start()
        self.loads += 1
        return copy

    def inside(self, block):
        return (block >= 0) & (block < self.count)

    def clamp(self, block):
        return jnp.clip(block, 0, self.count - 1)

    def slab_of(self, index):
        return pl.ds(pl.multiple_of(index * self.slab, self.slab), self.slab)


    def kv_spot(self, block, which, half):
        first = block * self.depth + which * self.piece + half * self.quarter
        return self.wkv.at[pl.ds(pl.multiple_of(first, self.quarter), self.quarter)]

    def begin(self):
        load = self.load
        self.load_kv = [
            load(
                self.kvw_in.at[
                    :,
                    pl.ds(
                        pl.multiple_of(
                            (kind * KEY_VALUE_HEADS + self.kv_head) * HEAD_WIDTH, HEAD_WIDTH
                        ),
                        HEAD_WIDTH,
                    ),
                ],
                self.wkv.at[self.own_rows, pl.ds(kind * HEAD_WIDTH, HEAD_WIDTH)],
            )
            for kind in range(2)
        ]
        self.load_decay = [
            load(self.decay_in, self.decay_ref),
            load(self.rate_in, self.rate_ref),
            load(self.beta_in, self.beta_ref),
        ]
        self.load_conv = [
            load(self.q_in, self.q_ref),
            load(self.k_in, self.k_ref),
            load(self.v_in, self.v_ref),
            load(self.cq_in, self.cq_ref),
            load(self.ck_in, self.ck_ref),
            load(self.cv_in, self.cv_ref),
        ]

        barrier = pltpu.get_barrier_semaphore()
        for axis, size, place in (
            ("seq", self.count, self.me),
            ("groups", self.groups, self.part),
            ("head", self.heads, self.lane),
        ):
            for e in range(1, size):
                pl.semaphore_signal(
                    barrier,
                    inc=1,
                    device_id={axis: lax.rem(place + e, size)},
                    device_id_type=MESH,
                )
        pl.semaphore_wait(barrier, self.count + self.groups + self.heads - 3)

        last = pl.ds(self.rows - TAIL, TAIL)
        self.tails = [
            remote(
                source.at[last],
                target,
                self.tail_send.at[i],
                self.tail_recv.at[i],
                "seq",
                self.follower,
            )
            for i, (source, target) in enumerate(
                (
                    (self.q_in, self.tail_q),
                    (self.k_in, self.tail_k),
                    (self.v_in, self.tail_v),
                )
            )
        ]

        @pl.when(self.me < self.count - 1)
        def _():
            for copy in self.tails:
                copy.start()

    def load_rest(self):
        load = self.load
        self.load_late = [
            load(self.gate_in, self.gate_ref),
            load(self.gain_in, self.gain_ref),
            load(self.ow_in, self.ow_ref),
            load(self.residual_in.at[self.slab_of(self.lane)], self.residual_ref),
            load(self.again_in, self.again_ref),
        ]

    def delta(self, pumps):
        rows, value_heads, share = self.rows, self.value_heads, self.share
        key_heads = self.key_heads
        for copy in self.load_decay:
            copy.wait()
        length = self.length_ref[0]
        at_row = self.me * rows + lax.broadcasted_iota(jnp.int32, (rows, value_heads), 0)
        alive = (at_row < length).astype(jnp.float32)
        beta = jax.nn.sigmoid(self.beta_ref[...]) * alive
        step = -self.rate_ref[...] * softplus(self.decay_ref[...]) * alive
        row = lax.broadcasted_iota(jnp.int32, (rows, rows), 0)
        column = lax.broadcasted_iota(jnp.int32, (rows, rows), 1)
        inclusive = row >= column
        run = exact(inclusive.astype(jnp.float32), step)
        run_t = exact(step, (row <= column).astype(jnp.float32), ((0,), (0,)))
        growth = jnp.exp(run)
        self.final = growth[rows - 1 : rows]
        ending_t = jnp.exp(run_t[:, rows - 1 : rows] - run_t)
        eye = (row == column).astype(jnp.float32)

        for copy in self.load_conv:
            copy.wait()
        q_width = key_heads * DK
        joined = self.joined
        joined[PAD:, :q_width] = self.q_ref[...].astype(jnp.float32)
        joined[PAD:, q_width : 2 * q_width] = self.k_ref[...].astype(jnp.float32)
        joined[PAD:, 2 * q_width :] = self.v_ref[...].astype(jnp.float32)

        @pl.when(self.me == 0)
        def _():
            self.enter[...] = jnp.zeros_like(self.enter)
            joined[:PAD] = jnp.zeros((PAD, joined.shape[1]), jnp.float32)

        @pl.when(self.me > 0)
        def _():
            for copy in self.tails:
                copy.wait_recv()
            joined[:PAD, :q_width] = self.tail_q[...].astype(jnp.float32)[TAIL - PAD :]
            joined[:PAD, q_width : 2 * q_width] = self.tail_k[...].astype(jnp.float32)[
                TAIL - PAD :
            ]
            joined[:PAD, 2 * q_width :] = self.tail_v[...].astype(jnp.float32)[TAIL - PAD :]

        def conv(base, taps, h):
            first_column = base + h * DK
            total = jnp.zeros((rows, DK), jnp.float32)
            for j in range(CONV):
                first = PAD - CONV + 1 + j
                total = total + taps[j : j + 1, h * DK : (h + 1) * DK] * joined[
                    first : first + rows, first_column : first_column + DK
                ]
            return total * jax.nn.sigmoid(total)

        queries, keyset, turned, grams = [], [], [], []
        for g in range(key_heads):
            q = unit(conv(0, self.cq_ref, g)) * DK ** (-0.5)
            k = unit(conv(q_width, self.ck_ref, g))
            k_t = k.T
            queries.append(q)
            keyset.append(k)
            turned.append(k_t)
            grams.append(mm(jnp.concatenate([k, q], 0), k_t))
        pumps[0]()

        mixes, lower, inverse = [], [], []
        for h in range(value_heads):
            spread = run[:, h : h + 1] - run_t[h : h + 1, :]
            w = jnp.exp(jnp.where(inclusive, spread, NEGATIVE))
            gram = grams[h // share]
            mixes.append((gram[rows:] * w).astype(jnp.bfloat16))
            low = jnp.where(row > column, beta[:, h : h + 1] * w * gram[:rows], 0.0)
            lower.append(low)
            pair = (row // 2 == column // 2) & (row > column)
            inverse.append(eye - jnp.where(pair, low, 0.0))
        size = 2
        while size < rows:
            off = (row // (2 * size) == column // (2 * size)) & (row // size > column // size)
            half = [mm(jnp.where(off, low, 0.0), x) for low, x in zip(lower, inverse)]
            inverse = [x - mm(x, y) for x, y in zip(inverse, half)]
            size *= 2
        pumps[1]()

        for h in range(value_heads):
            k = keyset[h // share]
            v = conv(2 * q_width, self.cv_ref, h)
            b = beta[:, h : h + 1]
            grown = growth[:, h : h + 1]
            wu = mm(inverse[h], jnp.concatenate([b * grown * k, b * v], 1))
            stop_t = (turned[h // share] * ending_t[h : h + 1, :]).astype(jnp.bfloat16)
            both = mm(jnp.concatenate([stop_t, mixes[h]], 0), wu)
            self.mapping[h, :DK] = both[:DK, :DK].astype(jnp.bfloat16)
            self.mapping[h, DK:] = (grown * queries[h // share] - both[DK:, :DK]).astype(
                jnp.bfloat16
            )
            self.injected[h] = both[:DK, DK:]
            self.local[h] = both[DK:, DK:]
        pumps[2]()

        for copy in self.load_late[:2]:
            copy.wait()
        self.states = []
        for h in range(value_heads):
            copy = remote(
                self.leave.at[h],
                self.enter.at[h],
                self.state_send.at[h],
                self.state_recv.at[h],
                "seq",
                self.follower,
            )
            self.states.append(copy)

            @pl.when(self.me > 0)
            def _():
                copy.wait_recv()

            state = self.enter[h]
            moved = mm(self.mapping[h], state)
            total = self.final[:, h : h + 1] * state.astype(jnp.float32)
            self.leave[h] = (total - moved[:DK] + self.injected[h]).astype(self.leave.dtype)
            o = self.local[h] + moved[DK:]
            scaled = (
                o * lax.rsqrt(jnp.mean(o * o, -1, keepdims=True) + EPSILON) * self.gain_ref[...]
            )
            gate = self.gate_ref[:, h * DV : (h + 1) * DV].astype(jnp.float32)
            self.gated[:, h * DV : (h + 1) * DV] = (
                scaled * (gate * jax.nn.sigmoid(gate))
            ).astype(self.gated.dtype)

            @pl.when(self.me < self.count - 1)
            def _():
                copy.start()

    def project_out(self):
        for copy in self.load_late[2:]:
            copy.wait()
        width = self.ow_ref.shape[1]
        tile = min(512, width)
        for c in range(0, width, tile):
            product = jnp.dot(
                self.gated[...],
                self.ow_ref[:, c : c + tile],
                preferred_element_type=jnp.float32,
            )
            self.summed[:, c : c + tile] = product
            self.partial[:, c : c + tile] = product.astype(self.partial.dtype)
        self.scatter = []
        for e in range(1, self.heads):
            peer = lax.rem(self.lane + e, self.heads)
            self.scatter.append(
                remote(
                    self.partial.at[self.slab_of(peer)],
                    self.landed.at[e - 1],
                    self.rs_send.at[e - 1],
                    self.rs_recv.at[e - 1],
                    "head",
                    peer,
                )
            )
        for copy in self.scatter:
            copy.start()

    def hidden_slab(self):
        for copy in self.scatter:
            copy.wait_recv()
        return self.residual_ref[...].astype(jnp.float32) + (
            self.summed[self.slab_of(self.lane)]
            + sum(self.landed[e].astype(jnp.float32) for e in range(self.heads - 1))
        )

    def gather_hidden(self, e, index):
        place = self.hidden.at[self.slab_of(index)]
        peer = lax.rem(self.lane + e, self.heads)
        return remote(
            place, place, self.ag_send.at[e - 1], self.ag_recv.at[e - 1], "head", peer
        )

    def send_hidden(self):
        for e in range(1, self.heads):
            self.gather_hidden(e, self.lane).start()

    def wait_hidden(self):
        for e in range(1, self.heads):
            self.gather_hidden(e, lax.rem(self.lane + self.heads - e, self.heads)).wait_recv()

    def scaled(self, hidden):
        widened = hidden.astype(jnp.float32)
        mean = jnp.mean(widened * widened, -1, keepdims=True)
        return (widened * lax.rsqrt(mean + EPSILON) * self.again_ref[...]).astype(jnp.bfloat16)

    def end(self):
        @pl.when(self.me < self.count - 1)
        def _():
            for copy in self.tails + self.states:
                copy.wait_send()

        for copy in self.scatter:
            copy.wait_send()
        for e in range(1, self.heads):
            self.gather_hidden(e, self.lane).wait_send()

    def attend(self, queries, keys, values, visible):
        scores = (
            lax.dot_general(
                queries, keys, (((1,), (1,)), ((), ())), preferred_element_type=jnp.float32
            )
            * HEAD_WIDTH ** (-0.5)
        )
        scores = jnp.where(visible, scores, NEGATIVE)
        peak = jnp.max(scores, -1, keepdims=True)
        weights = jnp.where(visible, jnp.exp(scores - peak), 0.0)
        norm = jnp.sum(weights, -1, keepdims=True)
        mixed = jnp.dot(weights.astype(jnp.bfloat16), values, preferred_element_type=jnp.float32)
        return mixed / norm


class Ring(Layer):
    def spot(self, block, which, half, u):
        if u == 0:
            return self.kv_spot(block, which, half)
        first = block * self.depth + which * self.piece
        return self.wq.at[u - 1, pl.ds(pl.multiple_of(first, self.piece), self.piece)]

    def along(self, d, j, u):
        sign = sign_of(d)
        block = self.clamp(self.me - sign * j)
        target = self.spot(block, self.part, self.core, u)
        source = target
        if j == 0 and u > 0:
            source = self.qw_in.at[
                pl.ds(pl.multiple_of(self.part * self.piece, self.piece), self.piece),
                pl.ds((u - 1) * 2 * HEAD_WIDTH, 2 * HEAD_WIDTH),
            ]
        copy = remote(
            source,
            target,
            self.z_send.at[d, j, u],
            self.z_recv.at[d, j, u],
            "seq",
            self.clamp(self.me + sign),
        )
        return copy, self.inside(self.me - sign * j) & self.inside(self.me + sign)

    def arriving(self, d, j, u):
        sign = sign_of(d)
        target = self.spot(self.clamp(self.me - sign * (j + 1)), self.part, self.core, u)
        copy = remote(
            target,
            target,
            self.z_send.at[d, j, u],
            self.z_recv.at[d, j, u],
            "seq",
            self.clamp(self.me + sign),
        )
        return copy, self.inside(self.me - sign * (j + 1))

    def across(self, e, d, j, u, which):
        target = self.spot(self.clamp(self.me - sign_of(d) * (j + 1)), which, self.core, u)
        return remote(
            target,
            target,
            self.y_send.at[e - 1, d, j, u],
            self.y_recv.at[e - 1, d, j, u],
            "groups",
            lax.rem(self.part + e, self.groups),
        )

    def beside(self, d, j, half):
        target = self.kv_spot(self.clamp(self.me - sign_of(d) * (j + 1)), self.part, half)
        return remote(target, target, self.m_send.at[d, j], self.m_recv.at[d, j], "head", self.mate)

    def source_of(self, e):
        return lax.rem(self.part + self.groups - e, self.groups)

    def beyond(self, e, d, j, half):
        target = self.kv_spot(self.clamp(self.me - sign_of(d) * (j + 1)), self.source_of(e), half)
        return remote(
            target,
            target,
            self.my_send.at[e - 1, d, j],
            self.my_recv.at[e - 1, d, j],
            "head",
            self.mate,
        )

    def onward(self, d, j, u):
        if j + 1 < self.count - 1:
            copy, go = self.along(d, j + 1, u)
            pl.when(go)(copy.start)

    def relay(self, d, j, u, forward=True):
        copy, here = self.arriving(d, j, u)

        @pl.when(here)
        def _():
            copy.wait_recv()
            for e in range(1, self.groups):
                self.across(e, d, j, u, self.part).start()
            if u == 0:
                self.beside(d, j, self.core).start()

        if forward:
            self.onward(d, j, u)

    def share_kv(self, d, j):
        _, here = self.arriving(d, j, 0)

        @pl.when(here)
        def _():
            for e in range(1, self.groups):
                self.across(e, d, j, 0, self.source_of(e)).wait_recv()
                self.beyond(e, d, j, self.core).start()

    def wait_kv(self, d, j):
        _, here = self.arriving(d, j, 0)

        @pl.when(here)
        def _():
            self.beside(d, j, 1 - self.core).wait_recv()
            for e in range(1, self.groups):
                self.beyond(e, d, j, 1 - self.core).wait_recv()

    def end_weights(self, units):
        for j in range(self.count - 1):
            for d in range(2):
                for u in range(units):
                    copy, go = self.along(d, j, u)
                    pl.when(go)(copy.wait_send)
                _, here = self.arriving(d, j, 0)

                @pl.when(here)
                def _():
                    for e in range(1, self.groups):
                        for u in range(units):
                            self.across(e, d, j, u, self.part).wait_send()
                        self.beyond(e, d, j, self.core).wait_send()
                    self.beside(d, j, self.core).wait_send()


def ring_kernel(sizes, names, *refs):
    s = Ring(sizes, names, refs)
    count, groups, me, rows = s.count, s.groups, s.me, s.rows
    units = s.query_heads + 1
    early = min(EARLY, units)
    s.begin()
    for copy in s.load_kv:
        copy.wait()
    for u in range(units):
        for d in range(2):
            if d == 1 or u < early:
                copy, go = s.along(d, 0, u)
                pl.when(go)(copy.start)
    s.load_rest()
    load_q = [
        s.load(
            s.qw_in.at[:, pl.ds(i * 2 * HEAD_WIDTH, 2 * HEAD_WIDTH)], s.wq.at[i, s.own_rows]
        )
        for i in range(s.query_heads)
    ]

    for b in range(1, count):

        @pl.when(b > me)
        def _():
            s.kvall[:, b * rows : (b + 1) * rows] = jnp.zeros(
                (2, rows, HEAD_WIDTH), s.kvall.dtype
            )

    def pump(u):
        def run():
            if u < early:
                for d in range(2):
                    s.relay(d, 0, u, forward=d == 1)

        return run

    s.delta([pump(u) for u in range(3)])
    for u in range(early, units):
        copy, go = s.along(0, 0, u)
        pl.when(go)(copy.start)
    for u in range(early):
        s.onward(0, 0, u)
    s.project_out()
    for u in range(early, units):
        for d in range(2):
            s.relay(d, 0, u)
    for d in range(2):
        s.share_kv(d, 0)
    s.hidden[s.slab_of(s.lane)] = s.hidden_slab().astype(s.hidden.dtype)
    s.send_hidden()
    for j in range(1, count - 1):
        for d in range(2):
            s.relay(d, j, 0)
    for j in range(1, count - 1):
        for d in range(2):
            s.share_kv(d, j)
    s.wait_hidden()
    save_hidden = s.load(s.hidden, s.hidden_out)
    s.normed[...] = s.scaled(s.hidden[...])

    for j in range(count - 1):
        for d in range(2):
            s.wait_kv(d, j)
    own_block = pl.ds(pl.multiple_of(me * rows, rows), rows)
    for kind in range(2):
        s.kvall[kind, own_block] = jnp.dot(
            s.normed[...],
            s.wkv[:, kind * HEAD_WIDTH : (kind + 1) * HEAD_WIDTH],
            preferred_element_type=jnp.float32,
        ).astype(s.kvall.dtype)

    def later(e, block, axis, index, kind, send, recv):
        place = s.kvall.at[kind, pl.ds(pl.multiple_of(s.clamp(block) * rows, rows), rows)]
        return remote(place, place, send.at[e - 1], recv.at[e - 1], axis, index)

    def sent_kv(e):
        return later(e, me, "seq", s.clamp(me + e), s.core, s.kv_send, s.kv_recv)

    def mate_kv(e, kind):
        return later(e, me - e, "head", s.mate, kind, s.km_send, s.km_recv)

    for e in range(1, count):
        pl.when(me + e < count)(sent_kv(e).start)

    for j in range(1, count - 1):
        for u in range(1, units):
            for d in range(2):
                if (j, u) < (count - 2, 1) or count == 2:
                    s.relay(d, j, u)

    for e in range(1, count):

        @pl.when(me >= e)
        def _():
            later(e, me - e, "seq", s.clamp(me - e), s.core, s.kv_send, s.kv_recv).wait_recv()
            mate_kv(e, s.core).start()

    for e in range(1, count):
        pl.when(me >= e)(mate_kv(e, 1 - s.core).wait_recv)

    for copy in load_q:
        copy.wait()
    keys_total = count * rows
    at_query = me * rows + lax.broadcasted_iota(jnp.int32, (rows, keys_total), 0)
    at_key = lax.broadcasted_iota(jnp.int32, (rows, keys_total), 1)
    visible = (at_key <= at_query) & (at_key < s.length_ref[0])
    for i in range(s.query_heads):
        if count > 2:
            for d in range(2):
                s.relay(d, count - 2, i + 1)
        for j in range(count - 1):
            for d in range(2):
                _, here = s.arriving(d, j, i + 1)

                @pl.when(here)
                def _():
                    for e in range(1, groups):
                        s.across(e, d, j, i + 1, s.source_of(e)).wait_recv()

        projected = jnp.dot(s.normed[...], s.wq[i], preferred_element_type=jnp.float32)
        mixed = s.attend(
            projected[:, :HEAD_WIDTH].astype(jnp.bfloat16), s.kvall[0], s.kvall[1], visible
        )
        s.attended[:, i * HEAD_WIDTH : (i + 1) * HEAD_WIDTH] = (
            mixed * jax.nn.sigmoid(projected[:, HEAD_WIDTH:])
        ).astype(s.attended.dtype)
    save_attended = s.load(s.attended, s.attention_out)

    s.end()
    s.end_weights(units)
    for e in range(1, count):
        pl.when(me + e < count)(sent_kv(e).wait_send)
        pl.when(me >= e)(mate_kv(e, s.core).wait_send)
    save_hidden.wait()
    save_attended.wait()


class Split(Ring):
    def weights(self, d, dist):
        sign = sign_of(d)
        peer = self.me + sign * dist
        wide = self.wq.shape[1]
        first = pl.multiple_of(self.part * self.piece, self.piece)
        target = pl.multiple_of(self.me * self.depth + self.part * self.piece, self.piece)
        copy = remote(
            self.qw_in.at[
                pl.ds(first, self.piece),
                pl.ds(pl.multiple_of(self.clamp(peer) * wide, wide), wide),
            ],
            self.wq.at[pl.ds(target, self.piece)],
            self.w_send.at[d, dist - 1],
            self.w_recv.at[d, dist - 1],
            "seq",
            self.clamp(peer),
        )
        return copy, self.inside(peer)

    def weights_across(self, e, d, dist, which):
        block = self.clamp(self.me - sign_of(d) * dist)
        first = pl.multiple_of(block * self.depth + which * self.piece, self.piece)
        place = self.wq.at[pl.ds(first, self.piece)]
        return remote(
            place,
            place,
            self.wy_send.at[e - 1, d, dist - 1],
            self.wy_recv.at[e - 1, d, dist - 1],
            "groups",
            lax.rem(self.part + e, self.groups),
        )

    def weights_relay(self, d, dist):
        block = self.me - sign_of(d) * dist
        first = self.clamp(block) * self.depth + self.part * self.piece
        place = self.wq.at[pl.ds(pl.multiple_of(first, self.piece), self.piece)]

        @pl.when(self.inside(block))
        def _():
            remote(
                place,
                place,
                self.w_send.at[d, dist - 1],
                self.w_recv.at[d, dist - 1],
                "seq",
                self.clamp(block),
            ).wait_recv()
            for e in range(1, self.groups):
                self.weights_across(e, d, dist, self.part).start()

    def weights_wait(self, d, dist):
        @pl.when(self.inside(self.me - sign_of(d) * dist))
        def _():
            for e in range(1, self.groups):
                self.weights_across(e, d, dist, self.source_of(e)).wait_recv()


    def place(self, block, index):
        first = block * self.rows + index * self.slab
        return self.every.at[pl.ds(pl.multiple_of(first, self.slab), self.slab)]

    def far(self, d, dist, block, index):
        place = self.place(self.clamp(block), self.lane)
        return remote(
            place,
            place,
            self.n_send.at[d, dist - 1],
            self.n_recv.at[d, dist - 1],
            "seq",
            self.clamp(index),
        )

    def near(self, d, dist, f, block, index):
        place = self.place(self.clamp(block), index)
        peer = lax.rem(self.lane + MATES * f, self.heads)
        return remote(
            place,
            place,
            self.x_send.at[d, dist, f - 1],
            self.x_recv.at[d, dist, f - 1],
            "head",
            peer,
        )

    def twin(self, d, dist, f, block, index):
        place = self.place(self.clamp(block), index)
        return remote(
            place, place, self.t_send.at[d, dist, f], self.t_recv.at[d, dist, f], "head", self.mate
        )

    def back(self, f, lane):
        return lax.rem(lane + self.heads - MATES * f, self.heads)

    def chips(self):
        return range(1, self.heads // MATES)

    def block_at(self, d, dist):
        return self.me - sign_of(d) * dist

    def steps(self, dist):
        return (0,) if dist == 0 else (0, 1)

    def rows_sent(self, dist):
        for d in self.steps(dist):
            block = self.block_at(d, dist)

            @pl.when(self.inside(block))
            def _():
                if dist > 0:
                    self.far(d, dist, block, block).wait_recv()
                for f in self.chips():
                    self.near(d, dist, f, block, self.lane).start()
                self.twin(d, dist, 0, block, self.lane).start()

    def rows_passed(self, dist):
        for d in self.steps(dist):
            block = self.block_at(d, dist)

            @pl.when(self.inside(block))
            def _():
                for f in self.chips():
                    self.near(d, dist, f, block, self.back(f, self.lane)).wait_recv()
                    self.twin(d, dist, f, block, self.back(f, self.lane)).start()

    def rows_ready(self, d, dist, block):
        for f in range(self.heads // MATES):
            self.twin(d, dist, f, block, self.back(f, self.mate)).wait_recv()

    def end_rows(self):
        for dist in range(self.count):
            for d in self.steps(dist):
                block = self.block_at(d, dist)
                if dist > 0:
                    peer = self.me + sign_of(d) * dist
                    pl.when(self.inside(peer))(self.far(d, dist, self.me, peer).wait_send)

                @pl.when(self.inside(block))
                def _():
                    for f in self.chips():
                        self.near(d, dist, f, block, self.lane).wait_send()
                    for f in range(self.heads // MATES):
                        self.twin(d, dist, f, block, self.back(f, self.lane)).wait_send()


def split_kernel(sizes, names, *refs):
    s = Split(sizes, names, refs)
    count, groups, me, rows = s.count, s.groups, s.me, s.rows
    wide = s.wq.shape[1]
    mine = wide // (2 * HEAD_WIDTH)
    s.begin()
    for copy in s.load_kv:
        copy.wait()
    for d in range(2):
        copy, go = s.along(d, 0, 0)
        pl.when(go)(copy.start)
    for dist in range(count - 1, 0, -1):
        for d in range(2):
            if d == 1 or dist > 1:
                copy, go = s.weights(d, dist)
                pl.when(go)(copy.start)
    s.load_rest()
    load_q = s.load(
        s.qw_in.at[:, pl.ds(pl.multiple_of(me * wide, wide), wide)], s.wq.at[s.own_rows]
    )

    def pump_first():
        for d in range(2):
            s.relay(d, 0, 0)

    def pump_second():
        for j in range(1, count - 1):
            for d in range(2):
                s.relay(d, j, 0)
        for d in range(2):
            s.share_kv(d, 0)

    def pump_third():
        s.weights_relay(1, 1)

    s.delta([pump_first, pump_second, pump_third])
    copy, go = s.weights(0, 1)
    pl.when(go)(copy.start)
    s.project_out()
    for j in range(1, count - 1):
        for d in range(2):
            s.share_kv(d, j)
    for dist in range(2, count):
        for d in range(2):
            s.weights_relay(d, dist)
    hidden = s.hidden_slab().astype(s.hidden.dtype)
    s.hidden[s.slab_of(s.lane)] = hidden
    s.every[pl.ds(pl.multiple_of(me * rows + s.lane * s.slab, s.slab), s.slab)] = s.scaled(hidden)
    for dist in range(1, count):
        for d in range(2):
            peer = me + sign_of(d) * dist
            pl.when(s.inside(peer))(s.far(d, dist, me, peer).start)
    s.rows_sent(0)
    s.weights_relay(0, 1)
    for j in range(count - 1):
        for d in range(2):
            s.wait_kv(d, j)
    load_q.wait()
    for dist in range(1, count):
        for d in range(2):
            s.weights_wait(d, dist)

    def project(block):
        at = pl.ds(pl.multiple_of(block * rows, rows), rows)
        x = s.every[at]
        for i in range(mine):
            first = i * 2 * HEAD_WIDTH
            query = jnp.dot(
                x, s.wq[:, first : first + HEAD_WIDTH], preferred_element_type=jnp.float32
            )
            gate = jnp.dot(
                x,
                s.wq[:, first + HEAD_WIDTH : first + 2 * HEAD_WIDTH],
                preferred_element_type=jnp.float32,
            )
            s.asked[i, at] = query.astype(jnp.bfloat16)
            s.opened[i, at] = jax.nn.sigmoid(gate)
        for kind in range(2):
            s.kvall[kind, at] = jnp.dot(
                x,
                s.wkv[:, kind * HEAD_WIDTH : (kind + 1) * HEAD_WIDTH],
                preferred_element_type=jnp.float32,
            ).astype(s.kvall.dtype)

    def project_at(dist):
        for d in s.steps(dist):
            block = s.block_at(d, dist)

            @pl.when(s.inside(block))
            def _():
                s.rows_ready(d, dist, block)
                project(block)

    s.rows_passed(0)
    for dist in range(1, count):
        s.rows_sent(dist)
        if dist > 1:
            s.rows_passed(dist - 1)
        project_at(dist - 1)
    s.send_hidden()
    s.rows_passed(count - 1)
    project_at(count - 1)

    span = mine * HEAD_WIDTH
    length = s.length_ref[0]

    def result(b, rank):
        return remote(
            s.attended.at[b],
            s.collected.at[:, pl.ds(pl.multiple_of(rank * span, span), span)],
            s.r_send.at[b],
            s.r_recv.at[rank],
            "seq",
            b,
        )

    for b in range(count):
        seen = (b + 1) * rows
        at_query = b * rows + lax.broadcasted_iota(jnp.int32, (rows, seen), 0)
        at_key = lax.broadcasted_iota(jnp.int32, (rows, seen), 1)
        visible = (at_key <= at_query) & (at_key < length)
        at = slice(b * rows, seen)
        for i in range(mine):
            mixed = s.attend(s.asked[i, at], s.kvall[0, :seen], s.kvall[1, :seen], visible)
            s.attended[b, :, i * HEAD_WIDTH : (i + 1) * HEAD_WIDTH] = (
                mixed * s.opened[i, at]
            ).astype(s.attended.dtype)

        @pl.when(me != b)
        def _():
            result(b, me).start()

        @pl.when(me == b)
        def _():
            s.collected[:, pl.ds(pl.multiple_of(me * span, span), span)] = s.attended[b]

    s.wait_hidden()
    save_hidden = s.load(s.hidden, s.hidden_out)
    for b in range(count):
        pl.when(me != b)(result(b, jnp.int32(b)).wait_recv)
    save_attended = s.load(s.collected, s.attention_out)

    for b in range(count):
        pl.when(me != b)(result(b, me).wait_send)
    s.end()
    s.end_weights(1)
    s.end_rows()
    for dist in range(1, count):
        for d in range(2):
            copy, go = s.weights(d, dist)
            pl.when(go)(copy.wait_send)

            @pl.when(s.inside(me - sign_of(d) * dist))
            def _():
                for e in range(1, groups):
                    s.weights_across(e, d, dist, s.part).wait_send()

    save_hidden.wait()
    save_attended.wait()


def shards(
    residual,
    query_in,
    key_in,
    value_in,
    gating_in,
    beta_logit,
    decay_logit,
    seq_length,
    conv_query,
    conv_key,
    conv_value,
    decay_rate,
    norm_gain,
    out_weight,
    attn_gain,
    query_weight,
    key_value_weight,
):
    count = lax.axis_size("seq")
    groups = lax.axis_size("groups")
    heads = lax.axis_size("head")
    rows, model = residual.shape
    value_heads = beta_logit.shape[1]
    query_heads = query_weight.shape[1] // (2 * HEAD_WIDTH)
    width = query_in.shape[1] + key_in.shape[1] + value_in.shape[1]
    depth = query_weight.shape[0] * count
    slab = rows // heads
    f32, bf16 = jnp.float32, jnp.bfloat16
    dma = pltpu.SemaphoreType.DMA
    anywhere = pl.BlockSpec(memory_space=pl.ANY)
    smem = pl.BlockSpec(memory_space=pltpu.SMEM)
    rate = decay_rate[None, :]
    gain = norm_gain[None, :]
    attn = attn_gain[None, :]
    like = lambda a: pltpu.VMEM(a.shape, a.dtype)
    split = query_heads % count == 0
    units = 1 if split else query_heads + 1
    scratch = dict(
        q_ref=like(query_in),
        k_ref=like(key_in),
        v_ref=like(value_in),
        gate_ref=like(gating_in),
        beta_ref=like(beta_logit),
        decay_ref=like(decay_logit),
        cq_ref=like(conv_query),
        ck_ref=like(conv_key),
        cv_ref=like(conv_value),
        rate_ref=like(rate),
        gain_ref=like(gain),
        ow_ref=like(out_weight),
        again_ref=like(attn),
        residual_ref=pltpu.VMEM((slab, model), bf16),
        wkv=pltpu.VMEM((depth, 2 * HEAD_WIDTH), bf16),
        tail_q=pltpu.VMEM((TAIL, query_in.shape[1]), bf16),
        tail_k=pltpu.VMEM((TAIL, key_in.shape[1]), bf16),
        tail_v=pltpu.VMEM((TAIL, value_in.shape[1]), bf16),
        joined=pltpu.VMEM((rows + PAD, width), f32),
        mapping=pltpu.VMEM((value_heads, DK + rows, DK), bf16),
        local=pltpu.VMEM((value_heads, rows, DV), f32),
        injected=pltpu.VMEM((value_heads, DK, DV), f32),
        enter=pltpu.VMEM((value_heads, DK, DV), bf16),
        leave=pltpu.VMEM((value_heads, DK, DV), bf16),
        gated=pltpu.VMEM((rows, value_heads * DV), bf16),
        summed=pltpu.VMEM((rows, model), f32),
        partial=pltpu.VMEM((rows, model), bf16),
        landed=pltpu.VMEM((heads - 1, slab, model), bf16),
        hidden=pltpu.VMEM((rows, model), bf16),
        kvall=pltpu.VMEM((2, count * rows, HEAD_WIDTH), bf16),
        load_sems=dma((24 + query_heads,)),
        tail_send=dma((3,)),
        tail_recv=dma((3,)),
        state_send=dma((value_heads,)),
        state_recv=dma((value_heads,)),
        z_send=dma((2, count - 1, units)),
        z_recv=dma((2, count - 1, units)),
        y_send=dma((groups - 1, 2, count - 1, units)),
        y_recv=dma((groups - 1, 2, count - 1, units)),
        m_send=dma((2, count - 1)),
        m_recv=dma((2, count - 1)),
        my_send=dma((groups - 1, 2, count - 1)),
        my_recv=dma((groups - 1, 2, count - 1)),
        rs_send=dma((heads - 1,)),
        rs_recv=dma((heads - 1,)),
        ag_send=dma((heads - 1,)),
        ag_recv=dma((heads - 1,)),
    )
    if split:
        mine = query_heads // count
        chips = heads // MATES
        scratch.update(
            wq=pltpu.VMEM((depth, mine * 2 * HEAD_WIDTH), bf16),
            every=pltpu.VMEM((count * rows, model), bf16),
            asked=pltpu.VMEM((mine, count * rows, HEAD_WIDTH), bf16),
            opened=pltpu.VMEM((mine, count * rows, HEAD_WIDTH), f32),
            attended=pltpu.VMEM((count, rows, mine * HEAD_WIDTH), bf16),
            collected=pltpu.VMEM((rows, query_heads * HEAD_WIDTH), bf16),
            w_send=dma((2, count - 1)),
            w_recv=dma((2, count - 1)),
            wy_send=dma((groups - 1, 2, count - 1)),
            wy_recv=dma((groups - 1, 2, count - 1)),
            n_send=dma((2, count - 1)),
            n_recv=dma((2, count - 1)),
            x_send=dma((2, count, chips - 1)),
            x_recv=dma((2, count, chips - 1)),
            t_send=dma((2, count, chips)),
            t_recv=dma((2, count, chips)),
            r_send=dma((count,)),
            r_recv=dma((count,)),
        )
    else:
        scratch.update(
            wq=pltpu.VMEM((query_heads, depth, 2 * HEAD_WIDTH), bf16),
            normed=pltpu.VMEM((rows, model), bf16),
            attended=pltpu.VMEM((rows, query_heads * HEAD_WIDTH), bf16),
            kv_send=dma((count - 1,)),
            kv_recv=dma((count - 1,)),
            km_send=dma((count - 1,)),
            km_recv=dma((count - 1,)),
        )
    return pl.pallas_call(
        functools.partial(
            split_kernel if split else ring_kernel,
            (count, groups, heads),
            INPUTS + OUTPUTS + list(scratch),
        ),
        out_shape=(
            jax.ShapeDtypeStruct(residual.shape, bf16),
            jax.ShapeDtypeStruct((rows, query_heads * HEAD_WIDTH), bf16),
        ),
        in_specs=[anywhere] * 7 + [smem] + [anywhere] * 9,
        out_specs=(anywhere, anywhere),
        scratch_shapes=list(scratch.values()),
        compiler_params=pltpu.CompilerParams(
            collective_id=0, has_side_effects=True, vmem_limit_bytes=56 * 2**20
        ),
        name="layer",
    )(
        residual,
        query_in,
        key_in,
        value_in,
        gating_in,
        beta_logit,
        decay_logit,
        seq_length,
        conv_query,
        conv_key,
        conv_value,
        rate,
        gain,
        out_weight,
        attn,
        query_weight,
        key_value_weight,
    )


def solution(mesh):
    placed = (
        P(("groups", "seq"), None),
        P(("groups", "seq"), "head"),
        P(("groups", "seq"), "head"),
        P(("groups", "seq"), "head"),
        P(("groups", "seq"), "head"),
        P(("groups", "seq"), "head"),
        P(("groups", "seq"), "head"),
        P("groups"),
        P(None, "head"),
        P(None, "head"),
        P(None, "head"),
        P("head"),
        P(),
        P("head", None),
        P(),
        P("seq", "head"),
        P("seq", None),
    )
    return jax.shard_map(
        shards,
        mesh=mesh,
        in_specs=placed,
        out_specs=(P(("groups", "seq"), None), P(("groups", "seq"), "head")),
        check_vma=False,
    )
```

time: 231 us -> 97.8 us (0.42)
  waiting for transfers between devices: 39.6 us -> 0 us
  Pallas kernels: 125 us -> 89.9 us
  blocking collectives: 15.5 us -> 0 us
  between operations: 16.3 us -> 1.29 us
  matrix products: 8.72 us -> 0 us
  other arithmetic: 7.15 us -> 0 us
  local copies, waits for them, and re-layouts: 12.7 us -> 6.38 us
  starting transfers between devices: 5.58 us -> 0 us
    psum x1 -> x0, waiting for transfers between devices: 39.6 us -> none  [shards(): lax.psum(jnp.dot(gated, out_weight, preferred_element_type=jnp.float32),...]
    pallas_call x1, Pallas kernels: 125 us -> 89.9 us  [shards(): pl.pallas_call(functools.partial(split_kernel if split else ring_kernel,...]
    all_gather x1 -> x0, blocking collectives: 15.5 us -> none  [shards(): lax.all_gather(kv_proj.astype(jnp.bfloat16), 'seq', axis=0, tiled=True)]
    dot_general x6 -> x0, matrix products: 8.72 us -> none  [the longest x1 5.75 us: shards(): jnp.dot(normalized, all_weights, preferred_element_type=jnp.float32)]
    ppermute x1 -> x0, starting transfers between devices: 5.54 us -> none  [shifted(): return lax.ppermute(shard, axis, pairs)]
    slice x10 -> x0, local copies, waits for them, and re-layouts: 3.44 us -> none  [the longest x3 2.3 us: delta(): tail = jnp.concatenate([q[rim:], k[rim:], v[rim:]], 1)]
    concatenate x3 -> x0, other arithmetic: 3.14 us -> none  [the longest x1 1.79 us: shards(): jnp.concatenate([query_weight, pick(key_value_weight, query_weight)], 1)]
    unnamed x36 -> x4, local copies, waits for them, and re-layouts: 7.38 us -> 6.38 us
  transfers between devices with their start and end apart: 2 -> 0, of which waited for: 1 -> 0; matrix products, arithmetic and copies ran while one was open for 2% -> 0% of each run, Pallas kernels for 0% -> 0%
where the time goes in v2:
time: 97.8 us; the launch traced here: 97.6 us
  Pallas kernels  89.9 us (92%)
  local copies, waits for them, and re-layouts  6.38 us (7%)
  between operations  1.29 us (1%)
    pallas_call x1, Pallas kernels, shards(): pl.pallas_call(functools.partial(split_kernel if split else ring_kernel,...  89.9 us
    unnamed x4, local copies, waits for them, and re-layouts  6.38 us

profile of v2, /device:TPU:0, one launch (start us, length us, event | category | flops | bytes accessed | tf_op | source)
XLA Modules:
  0.0 97.6 jit_solution(2319169990843614164)
XLA Ops:
  1.3 1.4 %copy.19.refs_5_ = f32[128,8]{1,0:T(8,128)} copy(f32[128,8]{0,1:T(8,128)} %param.22) | data formatting | bytes 8192 | tf_op args[5]
  2.7 1.4 %copy.20.refs_6_ = f32[128,8]{1,0:T(8,128)} copy(f32[128,8]{0,1:T(8,128)} %param.23) | data formatting | bytes 8192 | tf_op args[6]
  4.1 89.9 %layer.1 = (bf16[128,2048]{1,0:T(8,128)(2,1)}, bf16[128,1024]{1,0:T(8,128)(2,1)}) custom-call(bf16[128,2048]{1,0:T(8,128)(2,1)} %refs_0_.1, bf16[128,512]{1,0:T(8,128)(2,1)} %refs_1_.1, bf16[128,512]{1,0:T(8,128)(2,1)} %refs_2_.1, bf16[128,1024]{1,0:T(8,128)(2,1)} %refs_3_.1, bf16[128,1024]{1,0:T(8,128)(2,1)} %refs_4_.1, f32[128,8]{1,0:T(8,128)} %copy.19.refs_5_, ...), custom_call_target="tpu_custom_call" | custom-call | tf_op jit(solution)/shard_map/layer/pallas_call | solution.py:1114
  94.0 1.9 %copy.24 = bf16[128,2048]{1,0:T(8,128)(2,1)} copy(bf16[128,2048]{1,0:T(8,128)(2,1)} %get-tuple-element.4) | data formatting | bytes 1048576
  95.9 1.7 %copy.25 = bf16[128,1024]{1,0:T(8,128)(2,1)} copy(bf16[128,1024]{1,0:T(8,128)(2,1)} %get-tuple-element.5) | data formatting | bytes 524288

commit v3 on v2

--- a/solution.py
+++ b/solution.py
@@ -17,6 +17,7 @@
 TAIL = 16
 MATES = 2
 EARLY = 3
+PIECES = 2
 
 EPSILON = 1e-06
 NEGATIVE = -1e30
@@ -214,15 +215,23 @@
         for copy in self.load_decay:
             copy.wait()
         length = self.length_ref[0]
-        at_row = self.me * rows + lax.broadcasted_iota(jnp.int32, (rows, value_heads), 0)
-        alive = (at_row < length).astype(jnp.float32)
-        beta = jax.nn.sigmoid(self.beta_ref[...]) * alive
-        step = -self.rate_ref[...] * softplus(self.decay_ref[...]) * alive
+        at = self.me * rows + lax.broadcasted_iota(jnp.int32, (value_heads, rows), 1)
+        alive = (at < length).astype(jnp.float32)
+        beta_t = jax.nn.sigmoid(self.beta_ref[...]) * alive
+        square = (value_heads, value_heads)
+        diagonal = lax.broadcasted_iota(jnp.int32, square, 0) == lax.broadcasted_iota(
+            jnp.int32, square, 1
+        )
+        rate = jnp.sum(jnp.where(diagonal, self.rate_ref[...], 0.0), -1, keepdims=True)
+        step_t = -rate * softplus(self.decay_ref[...]) * alive
         row = lax.broadcasted_iota(jnp.int32, (rows, rows), 0)
         column = lax.broadcasted_iota(jnp.int32, (rows, rows), 1)
         inclusive = row >= column
-        run = exact(inclusive.astype(jnp.float32), step)
-        run_t = exact(step, (row <= column).astype(jnp.float32), ((0,), (0,)))
+        run_t = exact(step_t, (row <= column).astype(jnp.float32))
+        blank = jnp.zeros((rows - 2 * value_heads, rows), jnp.float32)
+        turned_over = jnp.concatenate([beta_t, run_t, blank], 0).T
+        beta = turned_over[:, :value_heads]
+        run = turned_over[:, value_heads : 2 * value_heads]
         growth = jnp.exp(run)
         self.final = growth[rows - 1 : rows]
         ending_t = jnp.exp(run_t[:, rows - 1 : rows] - run_t)
@@ -270,7 +279,9 @@
             keyset.append(k)
             turned.append(k_t)
             grams.append(mm(jnp.concatenate([k, q], 0), k_t))
-        pumps[0]()
+            if g == key_heads // 2 - 1:
+                pumps[0]()
+        pumps[1]()
 
         mixes, lower, inverse = [], [], []
         for h in range(value_heads):
@@ -288,7 +299,7 @@
             half = [mm(jnp.where(off, low, 0.0), x) for low, x in zip(lower, inverse)]
             inverse = [x - mm(x, y) for x, y in zip(inverse, half)]
             size *= 2
-        pumps[1]()
+        pumps[2]()
 
         for h in range(value_heads):
             k = keyset[h // share]
@@ -304,12 +315,13 @@
             )
             self.injected[h] = both[:DK, DK:]
             self.local[h] = both[DK:, DK:]
-        pumps[2]()
-
+        pumps[3]()
+
+    def chain(self):
         for copy in self.load_late[:2]:
             copy.wait()
         self.states = []
-        for h in range(value_heads):
+        for h in range(self.value_heads):
             copy = remote(
                 self.leave.at[h],
                 self.enter.at[h],
@@ -512,6 +524,10 @@
         if forward:
             self.onward(d, j, u)
 
+    def kv_relays(self, d, first, last):
+        for j in range(max(first, 1), last):
+            self.relay(d, j, 0)
+
     def share_kv(self, d, j):
         _, here = self.arriving(d, j, 0)
 
@@ -584,7 +600,8 @@
 
         return run
 
-    s.delta([pump(u) for u in range(3)])
+    s.delta([lambda: None] + [pump(u) for u in range(3)])
+    s.chain()
     for u in range(early, units):
         copy, go = s.along(0, 0, u)
         pl.when(go)(copy.start)
@@ -686,77 +703,86 @@
 
 
 class Split(Ring):
-    def weights(self, d, dist):
+    def weights(self, d, dist, p):
         sign = sign_of(d)
         peer = self.me + sign * dist
         wide = self.wq.shape[1]
-        first = pl.multiple_of(self.part * self.piece, self.piece)
-        target = pl.multiple_of(self.me * self.depth + self.part * self.piece, self.piece)
+        size = self.piece // PIECES
+        first = pl.multiple_of(self.part * self.piece + p * size, size)
         copy = remote(
             self.qw_in.at[
-                pl.ds(first, self.piece),
+                pl.ds(first, size),
                 pl.ds(pl.multiple_of(self.clamp(peer) * wide, wide), wide),
             ],
-            self.wq.at[pl.ds(target, self.piece)],
-            self.w_send.at[d, dist - 1],
-            self.w_recv.at[d, dist - 1],
+            self.weight_rows(self.me, self.part, p),
+            self.w_send.at[d, dist - 1, p],
+            self.w_recv.at[d, dist - 1, p],
             "seq",
             self.clamp(peer),
         )
         return copy, self.inside(peer)
 
-    def weights_across(self, e, d, dist, which):
-        block = self.clamp(self.me - sign_of(d) * dist)
-        first = pl.multiple_of(block * self.depth + which * self.piece, self.piece)
-        place = self.wq.at[pl.ds(first, self.piece)]
+    def weight_rows(self, block, which, p):
+        size = self.piece // PIECES
+        first = self.clamp(block) * self.depth + which * self.piece + p * size
+        return self.wq.at[pl.ds(pl.multiple_of(first, size), size)]
+
+    def weights_across(self, e, d, dist, which, p):
+        place = self.weight_rows(self.me - sign_of(d) * dist, which, p)
         return remote(
             place,
             place,
-            self.wy_send.at[e - 1, d, dist - 1],
-            self.wy_recv.at[e - 1, d, dist - 1],
+            self.wy_send.at[e - 1, d, dist - 1, p],
+            self.wy_recv.at[e - 1, d, dist - 1, p],
             "groups",
             lax.rem(self.part + e, self.groups),
         )
 
     def weights_relay(self, d, dist):
         block = self.me - sign_of(d) * dist
-        first = self.clamp(block) * self.depth + self.part * self.piece
-        place = self.wq.at[pl.ds(pl.multiple_of(first, self.piece), self.piece)]
 
         @pl.when(self.inside(block))
         def _():
-            remote(
-                place,
-                place,
-                self.w_send.at[d, dist - 1],
-                self.w_recv.at[d, dist - 1],
-                "seq",
-                self.clamp(block),
-            ).wait_recv()
-            for e in range(1, self.groups):
-                self.weights_across(e, d, dist, self.part).start()
+            for p in range(PIECES):
+                place = self.weight_rows(block, self.part, p)
+                remote(
+                    place,
+                    place,
+                    self.w_send.at[d, dist - 1, p],
+                    self.w_recv.at[d, dist - 1, p],
+                    "seq",
+                    self.clamp(block),
+                ).wait_recv()
+                for e in range(1, self.groups):
+                    self.weights_across(e, d, dist, self.part, p).start()
 
     def weights_wait(self, d, dist):
         @pl.when(self.inside(self.me - sign_of(d) * dist))
         def _():
             for e in range(1, self.groups):
-                self.weights_across(e, d, dist, self.source_of(e)).wait_recv()
+                for p in range(PIECES):
+                    self.weights_across(e, d, dist, self.source_of(e), p).wait_recv()
 
 
     def place(self, block, index):
         first = block * self.rows + index * self.slab
         return self.every.at[pl.ds(pl.multiple_of(first, self.slab), self.slab)]
 
-    def far(self, d, dist, block, index):
+    def far(self, d, dist, block):
         place = self.place(self.clamp(block), self.lane)
         return remote(
             place,
             place,
-            self.n_send.at[d, dist - 1],
-            self.n_recv.at[d, dist - 1],
+            self.n_send.at[d, dist],
+            self.n_recv.at[d, dist],
             "seq",
-            self.clamp(index),
-        )
+            self.clamp(self.me + sign_of(d)),
+        )
+
+    def rows_onward(self, d, dist):
+        block = self.me - sign_of(d) * dist
+        go = self.inside(block) & self.inside(self.me + sign_of(d))
+        return self.far(d, dist, block), go
 
     def near(self, d, dist, f, block, index):
         place = self.place(self.clamp(block), index)
@@ -788,39 +814,42 @@
     def steps(self, dist):
         return (0,) if dist == 0 else (0, 1)
 
-    def rows_sent(self, dist):
-        for d in self.steps(dist):
-            block = self.block_at(d, dist)
-
-            @pl.when(self.inside(block))
-            def _():
-                if dist > 0:
-                    self.far(d, dist, block, block).wait_recv()
-                for f in self.chips():
-                    self.near(d, dist, f, block, self.lane).start()
-                self.twin(d, dist, 0, block, self.lane).start()
-
-    def rows_passed(self, dist):
-        for d in self.steps(dist):
-            block = self.block_at(d, dist)
-
-            @pl.when(self.inside(block))
-            def _():
-                for f in self.chips():
-                    self.near(d, dist, f, block, self.back(f, self.lane)).wait_recv()
-                    self.twin(d, dist, f, block, self.back(f, self.lane)).start()
+    def rows_sent(self, d, dist):
+        block = self.block_at(d, dist)
+
+        @pl.when(self.inside(block))
+        def _():
+            if dist > 0:
+                self.far(d, dist - 1, block).wait_recv()
+            for f in self.chips():
+                self.near(d, dist, f, block, self.lane).start()
+            self.twin(d, dist, 0, block, self.lane).start()
+
+        if 0 < dist < self.count - 1:
+            copy, go = self.rows_onward(d, dist)
+            pl.when(go)(copy.start)
+
+    def rows_passed(self, d, dist):
+        block = self.block_at(d, dist)
+
+        @pl.when(self.inside(block))
+        def _():
+            for f in self.chips():
+                self.near(d, dist, f, block, self.back(f, self.lane)).wait_recv()
+                self.twin(d, dist, f, block, self.back(f, self.lane)).start()
 
     def rows_ready(self, d, dist, block):
         for f in range(self.heads // MATES):
             self.twin(d, dist, f, block, self.back(f, self.mate)).wait_recv()
 
     def end_rows(self):
+        for dist in range(self.count - 1):
+            for d in range(2):
+                copy, go = self.rows_onward(d, dist)
+                pl.when(go)(copy.wait_send)
         for dist in range(self.count):
             for d in self.steps(dist):
                 block = self.block_at(d, dist)
-                if dist > 0:
-                    peer = self.me + sign_of(d) * dist
-                    pl.when(self.inside(peer))(self.far(d, dist, self.me, peer).wait_send)
 
                 @pl.when(self.inside(block))
                 def _():
@@ -836,61 +865,105 @@
     wide = s.wq.shape[1]
     mine = wide // (2 * HEAD_WIDTH)
     s.begin()
+    last = count - 1
+
+    def send_weights(d, dist):
+        for p in range(PIECES):
+            copy, go = s.weights(d, dist, p)
+            pl.when(go)(copy.start)
+
     for copy in s.load_kv:
         copy.wait()
     for d in range(2):
         copy, go = s.along(d, 0, 0)
         pl.when(go)(copy.start)
-    for dist in range(count - 1, 0, -1):
-        for d in range(2):
-            if d == 1 or dist > 1:
-                copy, go = s.weights(d, dist)
-                pl.when(go)(copy.start)
+    pl.when(me > 0)(functools.partial(send_weights, 0, 1))
     s.load_rest()
     load_q = s.load(
         s.qw_in.at[:, pl.ds(pl.multiple_of(me * wide, wide), wide)], s.wq.at[s.own_rows]
     )
 
-    def pump_first():
-        for d in range(2):
-            s.relay(d, 0, 0)
-
-    def pump_second():
-        for j in range(1, count - 1):
-            for d in range(2):
-                s.relay(d, j, 0)
-        for d in range(2):
-            s.share_kv(d, 0)
-
-    def pump_third():
-        s.weights_relay(1, 1)
-
-    s.delta([pump_first, pump_second, pump_third])
-    copy, go = s.weights(0, 1)
-    pl.when(go)(copy.start)
+    def pump_heads():
+        @pl.when(me > 0)
+        def _():
+            s.relay(0, 0, 0, forward=False)
+            s.relay(1, 0, 0)
+            send_weights(1, 1)
+
+    def pump_updates():
+        @pl.when(me > 0)
+        def _():
+            for j in range(1, last - 1):
+                s.relay(1, j, 0)
+
+        pl.when(me > 1)(functools.partial(s.weights_relay, 0, 1))
+        for dist in range(2, count):
+            send_weights(1, dist)
+
+    s.delta([pump_heads, lambda: None, lambda: None, pump_updates])
+    s.chain()
+    s.onward(0, 0, 0)
     s.project_out()
-    for j in range(1, count - 1):
-        for d in range(2):
-            s.share_kv(d, j)
-    for dist in range(2, count):
-        for d in range(2):
-            s.weights_relay(d, dist)
+    s.kv_relays(0, 1, last - 1)
     hidden = s.hidden_slab().astype(s.hidden.dtype)
     s.hidden[s.slab_of(s.lane)] = hidden
     s.every[pl.ds(pl.multiple_of(me * rows + s.lane * s.slab, s.slab), s.slab)] = s.scaled(hidden)
-    for dist in range(1, count):
+    for d in range(2):
+        copy, go = s.rows_onward(d, 0)
+        pl.when(go)(copy.start)
+    s.rows_sent(0, 0)
+
+    s.rows_sent(0, 1)
+
+    def send_far():
+        for dist in range(last, 1, -1):
+            send_weights(0, dist)
+
+    @pl.when(me == 0)
+    def _():
+        send_weights(0, 1)
+        s.relay(1, 0, 0)
+
+    pl.when(me == 1)(functools.partial(s.weights_relay, 0, 1))
+    pl.when(me > 0)(send_far)
+    s.weights_relay(1, 1)
+    for d in range(2):
+        s.share_kv(d, 0)
+    pl.when(me == 0)(functools.partial(s.kv_relays, 1, 1, last - 1))
+    for d in range(2):
+        s.kv_relays(d, last - 1, last)
+
+    def far_weights(d):
+        for dist in range(last - 1, 1, -1):
+            s.weights_relay(d, dist)
+
+    pl.when(me > 0)(functools.partial(far_weights, 1))
+    s.rows_passed(0, 0)
+
+    @pl.when(me == 0)
+    def _():
+        s.weights_relay(1, last)
+        send_far()
+
+    s.rows_sent(1, 1)
+    for dist in range(2, last):
+        s.rows_sent(0, dist)
+    s.rows_passed(0, 1)
+    for j in range(1, last):
         for d in range(2):
-            peer = me + sign_of(d) * dist
-            pl.when(s.inside(peer))(s.far(d, dist, me, peer).start)
-    s.rows_sent(0)
-    s.weights_relay(0, 1)
-    for j in range(count - 1):
-        for d in range(2):
-            s.wait_kv(d, j)
-    load_q.wait()
-    for dist in range(1, count):
-        for d in range(2):
-            s.weights_wait(d, dist)
+            s.share_kv(d, j)
+    s.weights_relay(0, last)
+    pl.when(me == 0)(functools.partial(far_weights, 1))
+    far_weights(0)
+    for dist in range(2, last):
+        s.rows_sent(1, dist)
+    s.rows_sent(0, last)
+    s.rows_passed(1, 1)
+    for dist in range(2, last):
+        s.rows_passed(0, dist)
+    s.rows_sent(1, last)
+    for dist in range(2, last):
+        s.rows_passed(1, dist)
 
     def project(block):
         at = pl.ds(pl.multiple_of(block * rows, rows), rows)
@@ -923,15 +996,19 @@
                 s.rows_ready(d, dist, block)
                 project(block)
 
-    s.rows_passed(0)
+    s.send_hidden()
+    for d in range(2):
+        s.rows_passed(d, last)
+    for j in range(last):
+        for d in range(2):
+            s.wait_kv(d, j)
+    load_q.wait()
     for dist in range(1, count):
-        s.rows_sent(dist)
-        if dist > 1:
-            s.rows_passed(dist - 1)
-        project_at(dist - 1)
-    s.send_hidden()
-    s.rows_passed(count - 1)
-    project_at(count - 1)
+        for d in range(2):
+            s.weights_wait(d, dist)
+    for dist in range(last):
+        project_at(dist)
+    project_at(last)
 
     span = mine * HEAD_WIDTH
     length = s.length_ref[0]
@@ -979,13 +1056,15 @@
     s.end_rows()
     for dist in range(1, count):
         for d in range(2):
-            copy, go = s.weights(d, dist)
-            pl.when(go)(copy.wait_send)
+            for p in range(PIECES):
+                copy, go = s.weights(d, dist, p)
+                pl.when(go)(copy.wait_send)
 
             @pl.when(s.inside(me - sign_of(d) * dist))
             def _():
                 for e in range(1, groups):
-                    s.weights_across(e, d, dist, s.part).wait_send()
+                    for p in range(PIECES):
+                        s.weights_across(e, d, dist, s.part, p).wait_send()
 
     save_hidden.wait()
     save_attended.wait()
@@ -1024,6 +1103,7 @@
     anywhere = pl.BlockSpec(memory_space=pl.ANY)
     smem = pl.BlockSpec(memory_space=pltpu.SMEM)
     rate = decay_rate[None, :]
+    beta_t, decay_t = beta_logit.T, decay_logit.T
     gain = norm_gain[None, :]
     attn = attn_gain[None, :]
     like = lambda a: pltpu.VMEM(a.shape, a.dtype)
@@ -1034,8 +1114,8 @@
         k_ref=like(key_in),
         v_ref=like(value_in),
         gate_ref=like(gating_in),
-        beta_ref=like(beta_logit),
-        decay_ref=like(decay_logit),
+        beta_ref=like(beta_t),
+        decay_ref=like(decay_t),
         cq_ref=like(conv_query),
         ck_ref=like(conv_key),
         cv_ref=like(conv_value),
@@ -1088,10 +1168,10 @@
             opened=pltpu.VMEM((mine, count * rows, HEAD_WIDTH), f32),
             attended=pltpu.VMEM((count, rows, mine * HEAD_WIDTH), bf16),
             collected=pltpu.VMEM((rows, query_heads * HEAD_WIDTH), bf16),
-            w_send=dma((2, count - 1)),
-            w_recv=dma((2, count - 1)),
-            wy_send=dma((groups - 1, 2, count - 1)),
-            wy_recv=dma((groups - 1, 2, count - 1)),
+            w_send=dma((2, count - 1, PIECES)),
+            w_recv=dma((2, count - 1, PIECES)),
+            wy_send=dma((groups - 1, 2, count - 1, PIECES)),
+            wy_recv=dma((groups - 1, 2, count - 1, PIECES)),
             n_send=dma((2, count - 1)),
             n_recv=dma((2, count - 1)),
             x_send=dma((2, count, chips - 1)),
@@ -1134,8 +1214,8 @@
         key_in,
         value_in,
         gating_in,
-        beta_logit,
-        decay_logit,
+        beta_t,
+        decay_t,
         seq_length,
         conv_query,
         conv_key,

time: 97.8 us -> 73.4 us (0.75)
  Pallas kernels: 89.9 us -> 68.3 us
  local copies, waits for them, and re-layouts: 6.38 us -> 3.55 us
    pallas_call x1, Pallas kernels: 89.9 us -> 68.3 us  [shards(): pl.pallas_call(functools.partial(split_kernel if split else ring_kernel,...]
    unnamed x4 -> x2, local copies, waits for them, and re-layouts: 6.38 us -> 3.55 us
where the time goes in v3:
time: 73.4 us; the launch traced here: 73.1 us
  Pallas kernels  68.3 us (93%)
  local copies, waits for them, and re-layouts  3.55 us (5%)
  between operations  1.29 us (2%)
    pallas_call x1, Pallas kernels, shards(): pl.pallas_call(functools.partial(split_kernel if split else ring_kernel,...  68.3 us
    unnamed x2, local copies, waits for them, and re-layouts  3.55 us

profile of v3, /device:TPU:0, one launch (start us, length us, event | category | flops | bytes accessed | tf_op | source)
XLA Modules:
  0.0 73.1 jit_solution(13326284912753748224)
XLA Ops:
  1.3 68.3 %layer.1 = (bf16[128,2048]{1,0:T(8,128)(2,1)}, bf16[128,1024]{1,0:T(8,128)(2,1)}) custom-call(bf16[128,2048]{1,0:T(8,128)(2,1)} %refs_0_.1, bf16[128,512]{1,0:T(8,128)(2,1)} %refs_1_.1, bf16[128,512]{1,0:T(8,128)(2,1)} %refs_2_.1, bf16[128,1024]{1,0:T(8,128)(2,1)} %refs_3_.1, bf16[128,1024]{1,0:T(8,128)(2,1)} %refs_4_.1, f32[8,128]{1,0:T(8,128)} %bitcast.6, ...), custom_call_target="tpu_custom_call" | custom-call | tf_op jit(solution)/shard_map/layer/pallas_call | solution.py:1194
  69.6 1.9 %copy.22 = bf16[128,2048]{1,0:T(8,128)(2,1)} copy(bf16[128,2048]{1,0:T(8,128)(2,1)} %get-tuple-element.4) | data formatting | bytes 1048576
  71.5 1.7 %copy.23 = bf16[128,1024]{1,0:T(8,128)(2,1)} copy(bf16[128,1024]{1,0:T(8,128)(2,1)} %get-tuple-element.5) | data formatting | bytes 524288

commit v4 on v3

--- a/solution.py
+++ b/solution.py
@@ -905,6 +905,8 @@
     s.onward(0, 0, 0)
     s.project_out()
     s.kv_relays(0, 1, last - 1)
+    for dist in range(1, last):
+        pl.when(me == dist)(functools.partial(s.rows_sent, 0, dist))
     hidden = s.hidden_slab().astype(s.hidden.dtype)
     s.hidden[s.slab_of(s.lane)] = hidden
     s.every[pl.ds(pl.multiple_of(me * rows + s.lane * s.slab, s.slab), s.slab)] = s.scaled(hidden)
@@ -913,11 +915,15 @@
         pl.when(go)(copy.start)
     s.rows_sent(0, 0)
 
-    s.rows_sent(0, 1)
-
     def send_far():
         for dist in range(last, 1, -1):
             send_weights(0, dist)
+
+    def far_weights(d):
+        for dist in range(last - 1, 1, -1):
+            s.weights_relay(d, dist)
+
+    pl.when((me != 1) & (me != last))(functools.partial(s.rows_sent, 0, 1))
 
     @pl.when(me == 0)
     def _():
@@ -925,19 +931,16 @@
         s.relay(1, 0, 0)
 
     pl.when(me == 1)(functools.partial(s.weights_relay, 0, 1))
+    s.weights_relay(1, 1)
     pl.when(me > 0)(send_far)
-    s.weights_relay(1, 1)
     for d in range(2):
         s.share_kv(d, 0)
     pl.when(me == 0)(functools.partial(s.kv_relays, 1, 1, last - 1))
     for d in range(2):
         s.kv_relays(d, last - 1, last)
-
-    def far_weights(d):
-        for dist in range(last - 1, 1, -1):
-            s.weights_relay(d, dist)
-
     pl.when(me > 0)(functools.partial(far_weights, 1))
+    if last > 1:
+        s.rows_sent(0, last)
     s.rows_passed(0, 0)
 
     @pl.when(me == 0)
@@ -945,28 +948,32 @@
         s.weights_relay(1, last)
         send_far()
 
+    if last > 1:
+        s.weights_relay(0, last)
+    pl.when(me == last)(functools.partial(s.rows_sent, 0, 1))
     s.rows_sent(1, 1)
-    for dist in range(2, last):
-        s.rows_sent(0, dist)
-    s.rows_passed(0, 1)
     for j in range(1, last):
         for d in range(2):
             s.share_kv(d, j)
-    s.weights_relay(0, last)
-    pl.when(me == 0)(functools.partial(far_weights, 1))
+    if last > 1:
+        s.rows_passed(0, last)
     far_weights(0)
     for dist in range(2, last):
+        pl.when(me != dist)(functools.partial(s.rows_sent, 0, dist))
+    pl.when(me == 0)(functools.partial(far_weights, 1))
+    for dist in range(2, last):
         s.rows_sent(1, dist)
-    s.rows_sent(0, last)
+    s.rows_passed(0, 1)
     s.rows_passed(1, 1)
     for dist in range(2, last):
         s.rows_passed(0, dist)
-    s.rows_sent(1, last)
+    if last > 1:
+        s.rows_sent(1, last)
     for dist in range(2, last):
         s.rows_passed(1, dist)
 
-    def project(block):
-        at = pl.ds(pl.multiple_of(block * rows, rows), rows)
+    def project(first, size):
+        at = pl.ds(pl.multiple_of(first, rows), size)
         x = s.every[at]
         for i in range(mine):
             first = i * 2 * HEAD_WIDTH
@@ -987,18 +994,20 @@
                 preferred_element_type=jnp.float32,
             ).astype(s.kvall.dtype)
 
-    def project_at(dist):
-        for d in s.steps(dist):
-            block = s.block_at(d, dist)
-
-            @pl.when(s.inside(block))
-            def _():
-                s.rows_ready(d, dist, block)
-                project(block)
+    upper = 2 * me >= count
+
+    def ready(far):
+        for dist in range(count):
+            for d in s.steps(dist):
+                block = s.block_at(d, dist)
+                end = jnp.where(upper, 0, last)
+                wanted = block == end if far else block != end
+
+                @pl.when(s.inside(block) & wanted)
+                def _():
+                    s.rows_ready(d, dist, block)
 
     s.send_hidden()
-    for d in range(2):
-        s.rows_passed(d, last)
     for j in range(last):
         for d in range(2):
             s.wait_kv(d, j)
@@ -1006,9 +1015,12 @@
     for dist in range(1, count):
         for d in range(2):
             s.weights_wait(d, dist)
-    for dist in range(last):
-        project_at(dist)
-    project_at(last)
+    ready(False)
+    project(jnp.where(upper, rows, 0), last * rows)
+    if last > 1:
+        s.rows_passed(1, last)
+    ready(True)
+    project(jnp.where(upper, 0, last * rows), rows)
 
     span = mine * HEAD_WIDTH
     length = s.length_ref[0]
@@ -1016,7 +1028,7 @@
     def result(b, rank):
         return remote(
             s.attended.at[b],
-            s.collected.at[:, pl.ds(pl.multiple_of(rank * span, span), span)],
+            s.attention_out.at[:, pl.ds(pl.multiple_of(rank * span, span), span)],
             s.r_send.at[b],
             s.r_recv.at[rank],
             "seq",
@@ -1039,15 +1051,14 @@
         def _():
             result(b, me).start()
 
-        @pl.when(me == b)
-        def _():
-            s.collected[:, pl.ds(pl.multiple_of(me * span, span), span)] = s.attended[b]
-
+    own = s.load(
+        s.attended.at[me],
+        s.attention_out.at[:, pl.ds(pl.multiple_of(me * span, span), span)],
+    )
     s.wait_hidden()
     save_hidden = s.load(s.hidden, s.hidden_out)
     for b in range(count):
         pl.when(me != b)(result(b, jnp.int32(b)).wait_recv)
-    save_attended = s.load(s.collected, s.attention_out)
 
     for b in range(count):
         pl.when(me != b)(result(b, me).wait_send)
@@ -1067,7 +1078,7 @@
                         s.weights_across(e, d, dist, s.part, p).wait_send()
 
     save_hidden.wait()
-    save_attended.wait()
+    own.wait()
 
 
 def shards(
@@ -1167,7 +1178,6 @@
             asked=pltpu.VMEM((mine, count * rows, HEAD_WIDTH), bf16),
             opened=pltpu.VMEM((mine, count * rows, HEAD_WIDTH), f32),
             attended=pltpu.VMEM((count, rows, mine * HEAD_WIDTH), bf16),
-            collected=pltpu.VMEM((rows, query_heads * HEAD_WIDTH), bf16),
             w_send=dma((2, count - 1, PIECES)),
             w_recv=dma((2, count - 1, PIECES)),
             wy_send=dma((groups - 1, 2, count - 1, PIECES)),

time: 73.4 us -> 70.3 us (0.958)
  Pallas kernels: 68.3 us -> 65.3 us
    pallas_call x1, Pallas kernels: 68.3 us -> 65.3 us  [shards(): pl.pallas_call(functools.partial(split_kernel if split else ring_kernel,...]
where the time goes in v4:
time: 70.3 us; the launch traced here: 70.1 us
  Pallas kernels  65.3 us (93%)
  local copies, waits for them, and re-layouts  3.55 us (5%)
  between operations  1.29 us (2%)
    pallas_call x1, Pallas kernels, shards(): pl.pallas_call(functools.partial(split_kernel if split else ring_kernel,...  65.3 us
    unnamed x2, local copies, waits for them, and re-layouts  3.55 us

profile of v4, /device:TPU:0, one launch (start us, length us, event | category | flops | bytes accessed | tf_op | source)
XLA Modules:
  0.0 70.1 jit_solution(1132127871110009199)
XLA Ops:
  1.3 65.3 %layer.1 = (bf16[128,2048]{1,0:T(8,128)(2,1)}, bf16[128,1024]{1,0:T(8,128)(2,1)}) custom-call(bf16[128,2048]{1,0:T(8,128)(2,1)} %refs_0_.1, bf16[128,512]{1,0:T(8,128)(2,1)} %refs_1_.1, bf16[128,512]{1,0:T(8,128)(2,1)} %refs_2_.1, bf16[128,1024]{1,0:T(8,128)(2,1)} %refs_3_.1, bf16[128,1024]{1,0:T(8,128)(2,1)} %refs_4_.1, f32[8,128]{1,0:T(8,128)} %bitcast.6, ...), custom_call_target="tpu_custom_call" | custom-call | tf_op jit(solution)/shard_map/layer/pallas_call | solution.py:1204
  66.6 1.9 %copy.22 = bf16[128,2048]{1,0:T(8,128)(2,1)} copy(bf16[128,2048]{1,0:T(8,128)(2,1)} %get-tuple-element.4) | data formatting | bytes 1048576
  68.5 1.7 %copy.23 = bf16[128,1024]{1,0:T(8,128)(2,1)} copy(bf16[128,1024]{1,0:T(8,128)(2,1)} %get-tuple-element.5) | data formatting | bytes 524288

commit v5 on v4

--- a/solution.py
+++ b/solution.py
@@ -14,7 +14,7 @@
 HEAD_WIDTH = 256
 CONV = 4
 PAD = 8
-TAIL = 16
+TAIL = 8
 MATES = 2
 EARLY = 3
 PIECES = 2
@@ -1079,6 +1079,19 @@
 
     save_hidden.wait()
     own.wait()
+
+
+def write_kernel(first_in, second_in, first_out, second_out, first, second, ins, outs):
+    pairs = ((first_in, first, first_out), (second_in, second, second_out))
+    reads = [pltpu.make_async_copy(a, b, ins.at[i]) for i, (a, b, _) in enumerate(pairs)]
+    writes = [pltpu.make_async_copy(b, c, outs.at[i]) for i, (_, b, c) in enumerate(pairs)]
+    for read in reads:
+        read.start()
+    for read, write in zip(reads, writes):
+        read.wait()
+        write.start()
+    for write in writes:
+        write.wait()
 
 
 def shards(
@@ -1201,7 +1214,7 @@
             km_send=dma((count - 1,)),
             km_recv=dma((count - 1,)),
         )
-    return pl.pallas_call(
+    results = pl.pallas_call(
         functools.partial(
             split_kernel if split else ring_kernel,
             (count, groups, heads),
@@ -1237,6 +1250,15 @@
         query_weight,
         key_value_weight,
     )
+    return pl.pallas_call(
+        write_kernel,
+        out_shape=tuple(jax.ShapeDtypeStruct(a.shape, a.dtype) for a in results),
+        in_specs=[anywhere] * 2,
+        out_specs=(anywhere, anywhere),
+        scratch_shapes=[like(a) for a in results] + [dma((2,)), dma((2,))],
+        compiler_params=pltpu.CompilerParams(vmem_limit_bytes=56 * 2**20),
+        name="write",
+    )(*results)
 
 
 def solution(mesh):

time: 70.3 us -> 68.3 us (0.972)
  local copies, waits for them, and re-layouts: 3.55 us -> 0 us
  Pallas kernels: 65.3 us -> 66.9 us
    unnamed x2 -> x0, local copies, waits for them, and re-layouts: 3.55 us -> none
    pallas_call x0 -> x1, Pallas kernels: none -> 1.95 us  [shards(): pl.pallas_call(write_kernel, out_shape=tuple((jax.ShapeDtypeStruct(a.shap...]
where the time goes in v5:
time: 68.3 us; the launch traced here: 68.1 us
  Pallas kernels  66.9 us (98%)
  between operations  1.29 us (2%)
    pallas_call x1, Pallas kernels, shards(): pl.pallas_call(functools.partial(split_kernel if split else ring_kernel,...  64.9 us
    pallas_call x1, Pallas kernels, shards(): pl.pallas_call(write_kernel, out_shape=tuple((jax.ShapeDtypeStruct(a.shap...  1.95 us

profile of v5, /device:TPU:0, one launch (start us, length us, event | category | flops | bytes accessed | tf_op | source)
XLA Modules:
  0.0 68.1 jit_solution(18346744278117738486)
XLA Ops:
  1.3 64.9 %layer.1 = (bf16[128,2048]{1,0:T(8,128)(2,1)}, bf16[128,1024]{1,0:T(8,128)(2,1)}) custom-call(bf16[128,2048]{1,0:T(8,128)(2,1)} %refs_0_.1, bf16[128,512]{1,0:T(8,128)(2,1)} %refs_1_.1, bf16[128,512]{1,0:T(8,128)(2,1)} %refs_2_.1, bf16[128,1024]{1,0:T(8,128)(2,1)} %refs_3_.1, bf16[128,1024]{1,0:T(8,128)(2,1)} %refs_4_.1, f32[8,128]{1,0:T(8,128)} %bitcast.6, ...), custom_call_target="tpu_custom_call" | custom-call | tf_op jit(solution)/shard_map/layer/pallas_call | solution.py:1217
  66.2 2.0 %write.1 = (bf16[128,2048]{1,0:T(8,128)(2,1)}, bf16[128,1024]{1,0:T(8,128)(2,1)}) custom-call(bf16[128,2048]{1,0:T(8,128)(2,1)} %get-tuple-element.4.first_in, bf16[128,1024]{1,0:T(8,128)(2,1)} %get-tuple-element.5.second_in), custom_call_target="tpu_custom_call" | custom-call | tf_op jit(solution)/shard_map/write/pallas_call | solution.py:1253

commit v6 on v5

--- a/solution.py
+++ b/solution.py
@@ -972,21 +972,25 @@
     for dist in range(2, last):
         s.rows_passed(1, dist)
 
-    def project(first, size):
-        at = pl.ds(pl.multiple_of(first, rows), size)
+    def project_query(first, size):
+        at = slice(first, first + size)
         x = s.every[at]
         for i in range(mine):
-            first = i * 2 * HEAD_WIDTH
+            left = i * 2 * HEAD_WIDTH
             query = jnp.dot(
-                x, s.wq[:, first : first + HEAD_WIDTH], preferred_element_type=jnp.float32
+                x, s.wq[:, left : left + HEAD_WIDTH], preferred_element_type=jnp.float32
             )
             gate = jnp.dot(
                 x,
-                s.wq[:, first + HEAD_WIDTH : first + 2 * HEAD_WIDTH],
+                s.wq[:, left + HEAD_WIDTH : left + 2 * HEAD_WIDTH],
                 preferred_element_type=jnp.float32,
             )
             s.asked[i, at] = query.astype(jnp.bfloat16)
             s.opened[i, at] = jax.nn.sigmoid(gate)
+
+    def project_kv(first, size):
+        at = slice(first, first + size)
+        x = s.every[at]
         for kind in range(2):
             s.kvall[kind, at] = jnp.dot(
                 x,
@@ -1011,16 +1015,38 @@
     for j in range(last):
         for d in range(2):
             s.wait_kv(d, j)
+
+    @pl.when(upper)
+    def _():
+        ready(True)
+        project_kv(0, rows)
+
+    @pl.when(jnp.logical_not(upper))
+    def _():
+        ready(False)
+        project_kv(0, last * rows)
+
     load_q.wait()
     for dist in range(1, count):
         for d in range(2):
             s.weights_wait(d, dist)
-    ready(False)
-    project(jnp.where(upper, rows, 0), last * rows)
+
+    @pl.when(upper)
+    def _():
+        project_query(0, rows)
+        ready(False)
+        project_kv(rows, last * rows)
+        project_query(rows, last * rows)
+
+    pl.when(jnp.logical_not(upper))(functools.partial(project_query, 0, last * rows))
     if last > 1:
         s.rows_passed(1, last)
-    ready(True)
-    project(jnp.where(upper, 0, last * rows), rows)
+
+    @pl.when(jnp.logical_not(upper))
+    def _():
+        ready(True)
+        project_kv(last * rows, rows)
+        project_query(last * rows, rows)
 
     span = mine * HEAD_WIDTH
     length = s.length_ref[0]

time: 68.3 us -> 67.6 us (0.990)
  Pallas kernels: 66.9 us -> 66.2 us
where the time goes in v6:
time: 67.6 us; the launch traced here: 67.5 us
  Pallas kernels  66.2 us (98%)
  between operations  1.29 us (2%)
    pallas_call x1, Pallas kernels, shards(): pl.pallas_call(functools.partial(split_kernel if split else ring_kernel,...  64.2 us
    pallas_call x1, Pallas kernels, shards(): pl.pallas_call(write_kernel, out_shape=tuple((jax.ShapeDtypeStruct(a.shap...  1.95 us

profile of v6, /device:TPU:0, one launch (start us, length us, event | category | flops | bytes accessed | tf_op | source)
XLA Modules:
  0.0 67.5 jit_solution(9278927396157293055)
XLA Ops:
  1.3 64.2 %layer.1 = (bf16[128,2048]{1,0:T(8,128)(2,1)}, bf16[128,1024]{1,0:T(8,128)(2,1)}) custom-call(bf16[128,2048]{1,0:T(8,128)(2,1)} %refs_0_.1, bf16[128,512]{1,0:T(8,128)(2,1)} %refs_1_.1, bf16[128,512]{1,0:T(8,128)(2,1)} %refs_2_.1, bf16[128,1024]{1,0:T(8,128)(2,1)} %refs_3_.1, bf16[128,1024]{1,0:T(8,128)(2,1)} %refs_4_.1, f32[8,128]{1,0:T(8,128)} %bitcast.6, ...), custom_call_target="tpu_custom_call" | custom-call | tf_op jit(solution)/shard_map/layer/pallas_call | solution.py:1243
  65.5 2.0 %write.1 = (bf16[128,2048]{1,0:T(8,128)(2,1)}, bf16[128,1024]{1,0:T(8,128)(2,1)}) custom-call(bf16[128,2048]{1,0:T(8,128)(2,1)} %get-tuple-element.4.first_in, bf16[128,1024]{1,0:T(8,128)(2,1)} %get-tuple-element.5.second_in), custom_call_target="tpu_custom_call" | custom-call | tf_op jit(solution)/shard_map/write/pallas_call | solution.py:1279
